TPU v7x, 256 devices: a whole 4x4x8 slice. The times are simulated.
256 devices in a mesh: tm: 32 (over z, x_lo, core), grp: 8 (over y, x_hi).
Axes of the slice: x: 4 (x_hi: 2, x_lo: 2; x = x_hi * 2 + x_lo), y: 4, z: 8, core: 2. Of those that a mesh axis runs over, the one named last changes fastest.
Arguments:
- residual: float32 [32, 8, 3072], P('tm', 'grp'), may hold values from -6 to 6
- weight: float32 [32, 8, 3072], P('tm', 'grp'), may hold values from 0.25 to 4
- source_part: float32 [5, 32, 8, 3072], P(None, 'tm', 'grp'), may hold values from -2.5 to 2.5
- source_index: int32 [32, 8, 3072], P('tm', 'grp'), may hold values from 0 to 4095
- source_delta: float32 [5, 32, 4096], P(None, 'tm'), may hold values from -6 to 6
- attitude_part: float32 [3, 32, 8, 3072], P(None, 'tm', 'grp'), may hold values from -6 to 6
- spline_phase: float32 [32, 8, 3072], P('tm', 'grp'), may hold values from 0 to 1
- knot_index: int32 [32, 8, 3072], P('tm', 'grp'), may hold values from 0 to 3071, as said below
- calib_part: float32 [6, 32, 8, 3072], P(None, 'tm', 'grp'), may hold values from -6 to 6
- calib_index: int32 [32, 8, 3072], P('tm', 'grp'), may hold values from 0 to 2047
- global_part: float32 [4, 32, 8, 3072], P(None, 'tm', 'grp'), may hold values from -6 to 6
Outputs:
- residual_new: float32 [32, 8, 3072], P('tm', 'grp')
- attitude_step: float32 [3, 3072], P(None, 'tm')
- calib_step: float32 [6, 2048], replicated
- global_step: float32 [4], replicated
Inputs may be any that keep to these rules, and one draw needn't show every extreme that they name: `knot_index`: observation r of interval t (in any group) lies in knot interval t * 96 + 4 * (r // 128) + j for some j in 0 .. 3.
All inputs are finite; a program needn't handle non-finite values.
Results may differ from a plain program's by a relative error of at most 0.00012.
Values sent between devices are 32-bit elements; how exact they have to be, the bound alone decides.
No kernel may reach another device: no remote copies, remote signals or barrier semaphores. Data moves between devices by JAX's collectives and lax.ppermute only.
A program may use at most 128 MiB of HBM per device.

v0:
```python
import math

import jax
import jax.numpy as jnp
from jax import lax
from jax.sharding import PartitionSpec as P

TILE = 128
KPT = 4
UNITS = 2048
CPAR = 6
GPAR = 4
ATT_SWEEPS = 4


OMEGA = 0.6
RIDGE = 1.0


def shifted(x, axis, by):
    count = lax.axis_size(axis)
    pairs = [(i, i + by) for i in range(count) if 0 <= i + by < count]
    return lax.ppermute(x, axis, pairs)


def from_everyone(x, axis):
    copies = jnp.broadcast_to(x, (lax.axis_size(axis), *x.shape))
    return lax.all_to_all(copies, axis, split_axis=0, concat_axis=0, tiled=True)


def taken_together(x, axis):
    return from_everyone(x, axis).sum(axis=0)


def padded_2(x, sides, width):
    for axis, dim in sides:
        count, length = (lax.axis_size(axis), x.shape[dim])
        up = [(i, (i + 1) % count) for i in range(count - 1)]
        down = [(j, i) for i, j in up]
        last = lax.slice_in_dim(x, length - width, length, axis=dim)
        leading = lax.slice_in_dim(x, 0, width, axis=dim)
        before = lax.ppermute(last, axis, up)
        after = lax.ppermute(leading, axis, down)
        x = jnp.concatenate([before, x, after], axis=dim)
    return x


def packed_total(arrays, axis):
    ravelled, at, outs = (jnp.concatenate([a.reshape(-1) for a in arrays]), 0, [])
    running = lax.psum(ravelled, axis)
    for a in arrays:
        outs.append(running[at : at + a.size].reshape(a.shape))
        at += a.size
    return tuple(outs)


def spline_basis(phase):
    inverse = 1.0 - phase
    square = phase * phase
    cubed = square * phase
    return [
        inverse * inverse * inverse / 6.0,
        (3.0 * cubed - 6.0 * square + 4.0) / 6.0,
        (-3.0 * cubed + 3.0 * square + 3.0 * phase + 1.0) / 6.0,
        cubed / 6.0,
    ]


def cholesky_lists(matrix, extent):
    lower_tri = [[None for column in range(extent)] for target in range(extent)]
    for column in range(extent):
        pivot_sq = matrix[column][column]
        for inner_k in range(column):
            pivot_sq = pivot_sq - lower_tri[column][inner_k] * lower_tri[column][inner_k]
        pivot_val = jnp.sqrt(pivot_sq)
        lower_tri[column][column] = pivot_val
        for target in range(column + 1, extent):
            entry_val = matrix[target][column]
            for inner_k in range(column):
                entry_val = entry_val - lower_tri[target][inner_k] * lower_tri[column][inner_k]
            lower_tri[target][column] = entry_val / pivot_val
    return lower_tri


def solve_lower(lower_tri, vector):
    result = []
    for target in range(len(vector)):
        running = vector[target]
        for inner_k in range(target):
            running = running - lower_tri[target][inner_k] * result[inner_k]
        result.append(running / lower_tri[target][target])
    return result


def solve_upper(lower_tri, vector):
    extent = len(vector)
    result = [None for target in range(extent)]
    for target in reversed(range(extent)):
        running = vector[target]
        for inner_k in range(target + 1, extent):
            running = running - lower_tri[inner_k][target] * result[inner_k]
        result[target] = running / lower_tri[target][target]
    return result


def upper_pairs(extent):
    return [(first, second) for first in range(extent) for second in range(first, extent)]


def symmetric_lists(upper_values, extent):
    matrix = [[None for second in range(extent)] for first in range(extent)]
    for position, index_pair in enumerate(upper_pairs(extent)):
        first, second = index_pair
        value_now = upper_values[position] + (RIDGE if first == second else 0.0)
        matrix[first][second] = value_now
        matrix[second][first] = value_now
    return matrix


def solve_blocks(upper_values, rhs_values, extent):
    lower_tri = cholesky_lists(symmetric_lists(upper_values, extent), extent)
    whitened = solve_lower(lower_tri, rhs_values)
    solution = solve_upper(lower_tri, whitened)
    return (jnp.stack(whitened), jnp.stack(solution))


def apply_band(band_own, band_left, padded):
    extent = band_own.shape[-1]
    result = padded[:, 3 : 3 + extent]
    for offset in range(4):
        ahead_x = padded[:, 3 + offset : 3 + offset + extent]
        result = result + jnp.sum(band_own[offset] * ahead_x[None, :, :], axis=1)
    for offset in range(1, 4):
        behind = padded[:, 3 - offset : 3 - offset + extent]
        blocks = band_left[offset][:, :, 3 - offset : 3 - offset + extent]
        result = result + jnp.sum(blocks * behind[:, None, :], axis=0)
    return result


def node_sweeps(band_own, band_left, rhs_att, extend):
    diagonal = [
        [band_own[0][first, second] + (RIDGE if first == second else 0.0) for second in range(3)]
        for first in range(3)
    ]
    lower_tri = cholesky_lists(diagonal, 3)

    def precondition(vector):
        return jnp.stack(
            solve_upper(lower_tri, solve_lower(lower_tri, [vector[axis_k] for axis_k in range(3)]))
        )

    answer = OMEGA * precondition(rhs_att)
    for sweep_no in range(1, ATT_SWEEPS):
        padded = extend(answer)
        answer = answer + OMEGA * precondition(rhs_att - apply_band(band_own, band_left, padded))
    padded = extend(answer)
    scaled = jnp.stack(
        [
            sum((lower_tri[inner_k][target] * answer[inner_k] for inner_k in range(target, 3)))
            for target in range(3)
        ]
    )
    return (answer, padded, scaled)


def node_features(vectors, weights, first_res, basis_no):
    term_list = []
    for offset in range(4 - basis_no):
        for first in range(3):
            for second in range(3):
                term_list.append(
                    weights * vectors[basis_no][first] * vectors[basis_no + offset][second]
                )
    for first in range(3):
        term_list.append(weights * vectors[basis_no][first] * first_res)
    return jnp.stack(term_list)


def spread_terms(stacked, basis_no):
    band_rows = (4 - basis_no) * 9
    filler = jnp.zeros((basis_no * 9,) + stacked.shape[1:], jnp.float32)
    return jnp.concatenate([stacked[:band_rows], filler, stacked[band_rows:]], axis=0)


def unit_matrix_terms(rows_part, weights):
    return [
        weights * rows_part[first] * rows_part[second]
        for first, second in upper_pairs(rows_part.shape[0])
    ]


def rhs_terms(rows_part, weights, resid_now):
    return [weights * rows_part[first] * resid_now for first in range(rows_part.shape[0])]


def bin_units(features, unit_ids):
    row_count = features.shape[1]
    block_rows = math.gcd(row_count, 1024)
    labels = jnp.arange(UNITS, dtype=jnp.int32)

    def add_block(step_no, running):
        start_at = step_no * block_rows
        feature_block = lax.dynamic_slice_in_dim(features, start_at, block_rows, 1)
        id_block = lax.dynamic_slice_in_dim(unit_ids, start_at, block_rows, 0)
        unit_table = (id_block[:, None] == labels[None, :]).astype(jnp.float32)
        return running + jnp.dot(
            feature_block,
            unit_table,
            precision=lax.Precision.HIGHEST,
            preferred_element_type=jnp.float32,
        )

    return lax.fori_loop(
        0, row_count // block_rows, add_block, jnp.zeros((features.shape[0], UNITS), jnp.float32)
    )


def per_device(
    residual,
    weight,
    source_part,
    source_index,
    source_delta,
    attitude_part,
    spline_phase,
    knot_index,
    calib_part,
    calib_index,
    global_part,
):
    row_count = residual.shape[-1]
    weights = weight.reshape(row_count)
    source_rows = source_part.reshape(5, row_count)
    picked = jnp.take(source_delta.reshape(5, -1), source_index.reshape(row_count), axis=1)
    first_res = residual.reshape(row_count) - jnp.sum(source_rows * picked, axis=0)
    basis_list = spline_basis(spline_phase.reshape(row_count))
    att_rows = attitude_part.reshape(3, row_count)
    vectors = [basis_val[None, :] * att_rows for basis_val in basis_list]
    tile_count = row_count // TILE
    nodes_dev = tile_count * KPT
    local_knot = knot_index.reshape(row_count) - lax.axis_index("tm") * nodes_dev
    slot_in_tile = (
        local_knot.reshape(tile_count, TILE)
        - KPT * jnp.arange(tile_count, dtype=jnp.int32)[:, None]
    )
    one_hot = (slot_in_tile[:, :, None] == jnp.arange(KPT, dtype=jnp.int32)[None, None, :]).astype(
        jnp.float32
    )
    calib_rows = calib_part.reshape(CPAR, row_count)
    global_rows = global_part.reshape(GPAR, row_count)
    unit_ids = calib_index.reshape(row_count)
    pair_count = CPAR * (CPAR + 1) // 2
    pair_global = GPAR * (GPAR + 1) // 2
    local_sums = jnp.zeros((39, nodes_dev + 3), jnp.float32)
    for basis_no in range(4):
        stacked = node_features(vectors, weights, first_res, basis_no)
        feature_count = stacked.shape[0]
        binned = jnp.einsum(
            "ftr,trq->ftq",
            stacked.reshape(feature_count, tile_count, TILE),
            one_hot,
            precision=lax.Precision.HIGHEST,
            preferred_element_type=jnp.float32,
        ).reshape(feature_count, nodes_dev)
        local_sums = local_sums + jnp.pad(
            spread_terms(binned, basis_no), ((0, 0), (basis_no, 3 - basis_no))
        )
    spill_in = shifted(local_sums[:, nodes_dev:], "tm", 1)
    own_sums = jnp.concatenate([local_sums[:, :3] + spill_in, local_sums[:, 3:nodes_dev]], axis=1)
    summed = taken_together(own_sums, "grp")
    band_own = summed[:36].reshape(4, 3, 3, -1)
    left_in = shifted(summed[:36, -3:], "tm", 1)
    band_left = jnp.concatenate([left_in.reshape(4, 3, 3, 3), band_own], axis=3)

    def extend_copy(vector):
        return padded_2(vector, (("tm", 1),), 3)

    answer, padded, attitude_step = node_sweeps(band_own, band_left, summed[36:], extend_copy)
    node_values = padded[:, 3:]
    second_res = first_res
    for basis_no in range(4):
        picked_nodes = jnp.take(node_values, local_knot + basis_no, axis=1)
        second_res = second_res - jnp.sum(vectors[basis_no] * picked_nodes, axis=0)
    both_units = bin_units(
        jnp.stack(
            unit_matrix_terms(calib_rows, weights) + rhs_terms(calib_rows, weights, second_res)
        ),
        unit_ids,
    )
    both_global = jnp.stack(
        [
            jnp.sum(term_row)
            for term_row in unit_matrix_terms(global_rows, weights)
            + rhs_terms(global_rows, weights, second_res)
        ]
    )
    both_units, both_global = packed_total((both_units, both_global), ("tm", "grp"))
    calib_step, calib_solution = solve_blocks(
        both_units[:pair_count], [both_units[pair_count + first] for first in range(CPAR)], CPAR
    )
    global_step, global_solution = solve_blocks(
        both_global[:pair_global], [both_global[pair_global + first] for first in range(GPAR)], GPAR
    )
    unit_values = jnp.take(calib_solution, unit_ids, axis=1)
    final_res = (
        second_res
        - jnp.sum(calib_rows * unit_values, axis=0)
        - jnp.sum(global_rows * global_solution[:, None], axis=0)
    )
    return (final_res.reshape(residual.shape), attitude_step, calib_step, global_step)


def solution(mesh):
    return jax.shard_map(
        per_device,
        mesh=mesh,
        in_specs=(
            P("tm", "grp", None),
            P("tm", "grp", None),
            P(None, "tm", "grp", None),
            P("tm", "grp", None),
            P(None, "tm", None),
            P(None, "tm", "grp", None),
            P("tm", "grp", None),
            P("tm", "grp", None),
            P(None, "tm", "grp", None),
            P("tm", "grp", None),
            P(None, "tm", "grp", None),
        ),
        out_specs=(P("tm", "grp", None), P(None, "tm"), P(), P()),
        check_vma=False,
    )
```

profile of v0, /device:TPU:1, one launch (start us, length us, event | category | flops | bytes accessed | tf_op | source)
XLA Modules:
  0.0 671.4 jit_solution(4870254680766041157)
XLA Ops:
  19.5 9.7 %gather_fusion = f32[3072,5]{1,0:T(8,128)S(1)} fusion(f32[5,4096]{0,1:T(8,128)} %bitcast.555, s32[3072]{0:T(1024)S(1)} %broadcast_clamp_fusion.1), kind=kCustom, calls=%fused_computation.4 | custom fusion | bytes 135168 | tf_op jit(solution)/shard_map/jit(_take)/gather | solution.py:234
  33.2 3.8 bitcast_multiply_fusion.8
  40.6 12.4 %multiply_reduce_fusion.33 = (f32[3072]{0:T(1024)}, f32[3072]{0:T(1024)S(1)}, f32[3072]{0:T(1024)S(1)}, f32[3072]{0:T(1024)S(1)}, f32[3072]{0:T(1024)S(1)}, /*in...) fusion(f32[1,3072]{0,1:T(8,128)S(1)} %get-tuple-element.423, ...), kind=kLoop, calls=%fused_computation.63 | loop fusion | flops 67584 | bytes 417792 | tf_op jit(solution)/shard_map/mul | solution.py:175
  53.0 10.3 %multiply_reduce_fusion.35 = (f32[3072]{0:T(1024)}, f32[3072]{0:T(1024)S(1)}, f32[3072]{0:T(1024)S(1)}, f32[3072]{0:T(1024)S(1)}, f32[3072]{0:T(1024)S(1)}, /*in...) fusion(f32[1,3072]{0,1:T(8,128)S(1)} %get-tuple-element.401, ...), kind=kLoop, calls=%fused_computation.65 | loop fusion | flops 58368 | bytes 368640 | tf_op jit(solution)/shard_map/mul | solution.py:175
  63.2 12.0 %multiply_reduce_fusion.60 = (f32[3072]{0:T(1024)}, f32[3072]{0:T(1024)}, f32[3072]{0:T(1024)}, f32[3072]{0:T(1024)}, f32[3072]{0:T(1024)}, /*index=5*/f32[3072]...) fusion(f32[1,3072]{0,1:T(8,128)S(1)} %get-tuple-element.402, ...), kind=kLoop, calls=%fused_computation.90 | loop fusion | flops 61440 | bytes 417792 | tf_op jit(solution)/shard_map/mul | solution.py:172
  77.2 15.1 %multiply_reduce_fusion.57 = (f32[3072]{0:T(1024)}, f32[3072]{0:T(1024)}, f32[3072]{0:T(1024)}, f32[3072]{0:T(1024)}, f32[3072]{0:T(1024)}, /*index=5*/f32[3072]...) fusion(f32[1,3072]{0,1:T(8,128)} %get-tuple-element.399, ...), kind=kLoop, calls=%fused_computation.87 | loop fusion | flops 55296 | bytes 393216 | tf_op jit(solution)/shard_map/mul | solution.py:172
  92.3 12.6 %multiply_reduce_fusion.54 = (f32[3072]{0:T(1024)}, f32[3072]{0:T(1024)}, f32[3072]{0:T(1024)}, f32[3072]{0:T(1024)}, f32[3072]{0:T(1024)}, /*index=5*/f32[3072]...) fusion(f32[1,3072]{0,1:T(8,128)S(1)} %copy-done.25, ...), kind=kLoop, calls=%fused_computation.84 | loop fusion | flops 55296 | bytes 393216 | tf_op jit(solution)/shard_map/mul | solution.py:172
  104.9 3.8 stack.538
  111.6 12.4 %multiply_reduce_fusion.75 = (f32[3072]{0:T(1024)S(1)}, f32[3072]{0:T(1024)S(1)}, f32[3072]{0:T(1024)S(1)}, f32[3072]{0:T(1024)S(1)}, f32[3072]{0:T(1024)S(1)}, ...) fusion(f32[1,3072]{0,1:T(8,128)} %get-tuple-element.403, ...), kind=kLoop, calls=%fused_computation.105 | loop fusion | flops 46080 | bytes 294912 | tf_op jit(solution)/shard_map/mul | solution.py:172
  124.1 7.6 %stack.507 = f32[39,24,128]{2,0,1:T(8,128)} concatenate(f32[1,24,128]{2,0,1:T(1,128)S(1)} %bitcast.608, f32[1,24,128]{2,0,1:T(1,128)S(1)} %bitcast.609, f32[1,24,128]{2,0,1:T(1,128)} %bitcast.610, f32[1,24,128]{2,0,1:T(1,128)S(1)} %bitcast.602, f32[1,24,128]{2,0,1:T(1,128)S(1)} %bitcast.603, f32[1,24,128]{2,0,1:T(1,128)S(1)} %bitcast.604, f32[1,24,128]{2,0,1:T(1,128)S(1)} %bitcast.605, ...), dimensions={0} | concatenate | bytes 958464 | tf_op jit(solution)/shard_map/stack | solution.py:176
  141.3 4.5 collective-permute-start
  150.9 6.4 all-to-all-start
  182.5 4.2 collective-permute-start.5
  190.0 4.2 collective-permute-start.7
  198.0 3.5 collective-permute-done.8
  201.7 11.1 %gather_fusion.5 = f32[3072,3]{1,0:T(8,128)} fusion(f32[3,99]{0,1:T(8,128)S(1)} %copy.791, s32[3072]{0:T(1024)S(1)} %get-tuple-element.485), kind=kCustom, calls=%fused_computation.3.clone | custom fusion | bytes 86016 | tf_op jit(solution)/shard_map/jit(_take)/gather | solution.py:282
  212.8 10.9 %gather_fusion.4 = f32[3072,3]{1,0:T(8,128)} fusion(f32[3,99]{0,1:T(8,128)S(1)} %copy.791, s32[3072]{0:T(1024)S(1)} %get-tuple-element.484), kind=kCustom, calls=%fused_computation.2.clone | custom fusion | bytes 86016 | tf_op jit(solution)/shard_map/jit(_take)/gather | solution.py:282
  223.7 10.9 %gather_fusion.3 = f32[3072,3]{1,0:T(8,128)} fusion(f32[3,99]{0,1:T(8,128)S(1)} %copy.791, s32[3072]{0:T(1024)S(1)} %get-tuple-element.483), kind=kCustom, calls=%fused_computation.1.clone | custom fusion | bytes 86016 | tf_op jit(solution)/shard_map/jit(_take)/gather | solution.py:282
  234.6 10.9 %gather_fusion.2 = f32[3072,3]{1,0:T(8,128)} fusion(f32[3,99]{0,1:T(8,128)S(1)} %copy.791, s32[3072]{0:T(1024)S(1)} %get-tuple-element.482), kind=kCustom, calls=%fused_computation.clone | custom fusion | bytes 86016 | tf_op jit(solution)/shard_map/jit(_take)/gather | solution.py:282
  245.5 5.1 fusion.10
  254.0 4.5 fusion.8
  261.9 5.4 multiply_multiply_fusion
  269.3 9.9 %multiply_multiply_fusion.2 = (f32[1,3072]{0,1:T(8,128)}, f32[1,3072]{0,1:T(8,128)}, f32[1,3072]{0,1:T(8,128)}, f32[1,3072]{0,1:T(8,128)}, f32[1,3072]{0,1:T(8,1...) fusion(f32[1,3072]{0,1:T(8,128)} %get-tuple-element.368, ...), kind=kLoop, calls=%fused_computation.147 | loop fusion | flops 52224 | bytes 270336 | tf_op jit(solution)/shard_map/mul | solution.py:193
  302.1 10.8 %fusion.121 = (f32[1,3072]{0,1:T(8,128)}, f32[1,3072]{0,1:T(8,128)}, f32[1,3072]{0,1:T(8,128)}, f32[1,3072]{0,1:T(8,128)}, f32[1,3072]{0,1:T(8,128)}, /*index=5*...) fusion(f32[1,3072]{0,1:T(8,128)} %get-tuple-element.415, ...), kind=kLoop, calls=%fused_computation.416 | loop fusion | flops 46080 | bytes 294912 | tf_op jit(solution)/shard_map/mul | solution.py:187
  337.2 11.7 %while.14 = (s32[]{:T(128)}, f32[27,2048]{1,0:T(8,128)S(1)}, f32[27,3072]{1,0:T(8,128)S(1)}, s32[3072]{0:T(1024)}, s32[]{:T(128)}, /*index=5*/s32[]{:T(128)}, s32[]{:T(128)}, s32[]{:T(128)}) while((s32[]{:T(128)}, f32[27,2048]{1,0:T(8,128)S(1)}, f32[27,3072]{1,0:T(8,128)S(1)}, s32[3072]{0:T(1024)}, s32[]{:T(128)}, ...), condition=%wide.region_28.30_spmd.clone, body=%wide.region_27.29_spmd.clone.sunk | while | flops 681684992 | bytes 626845 | solution.py:213
  337.9 3.2 fusion.141
  341.8 3.2 fusion.141
  345.7 3.2 fusion.141
  349.8 19.8 %concatenate.95 = f32[55310]{0:T(1024)} concatenate(f32[55296]{0:T(1024)S(1)} %reshape.2027, f32[1]{0:T(128)} %bitcast.160, f32[1]{0:T(128)} %bitcast.162, f32[1]{0:T(128)} %bitcast.164, f32[1]{0:T(128)} %bitcast.166, f32[1]{0:T(128)} %bitcast.167, f32[1]{0:T(128)} %bitcast.168, f32[1]{0:T(128)} %bitcast.169, f32[1]{0:T(128)} %bitcast.170, f32[1]{0:T(128)} %bitcast.171, ...), dimensions={0} | concatenate | bytes 442480 | tf_op jit(solution)/shard_map/concatenate | solution.py:49
  370.2 263.2 %all-reduce.6.cloned.1.call-done = f32[55310]{0:T(1024)} async-done(((f32[55310]{0:T(1024)}), f32[55310]{0:T(1024)}) %all-reduce.6.cloned.1.call-update) | async-done | bytes 221256 | tf_op jit(solution)/shard_map/psum | solution.py:50
  647.4 10.8 %gather_fusion.1 = f32[3072,6]{1,0:T(8,128)} fusion(f32[6,2048]{0,1:T(8,128)S(1)} %copy.860, s32[3072]{0:T(1024)S(1)} %broadcast_clamp_fusion), kind=kCustom, calls=%fused_computation.5 | custom fusion | bytes 159744 | tf_op jit(solution)/shard_map/jit(_take)/gather | solution.py:304
  658.2 3.2 fusion.7
  (377 shorter events, 137.5 us)
Async XLA Ops:
  37.0 26.2 %copy-start = (f32[3,3072]{0,1:T(8,128)}, f32[3,3072]{0,1:T(8,128)S(1)}, u32[]{:S(2)}) copy-start(f32[3,3072]{0,1:T(8,128)S(1)} %get-tuple-element.442) | copy-start | bytes 110596
  37.0 26.2 %copy-start.5 = (f32[3,3072]{0,1:T(8,128)}, f32[3,3072]{0,1:T(8,128)S(1)}, u32[]{:S(2)}) copy-start(f32[3,3072]{0,1:T(8,128)S(1)} %get-tuple-element.441) | copy-start | bytes 110596
  77.2 15.2 %copy-start.1 = (f32[3,3072]{0,1:T(8,128)S(1)}, f32[3,3072]{0,1:T(8,128)}, u32[]{:S(2)}) copy-start(f32[3,3072]{0,1:T(8,128)} %copy-done) | copy-start | bytes 110596
  77.2 15.2 %copy-start.3 = (f32[1,3072]{0,1:T(8,128)S(1)}, f32[1,3072]{0,1:T(8,128)}, u32[]{:S(2)}) copy-start(f32[1,3072]{0,1:T(8,128)} %copy.664) | copy-start | bytes 36868
  77.2 15.2 %copy-start.6 = (f32[3,3072]{0,1:T(8,128)S(1)}, f32[3,3072]{0,1:T(8,128)}, u32[]{:S(2)}) copy-start(f32[3,3072]{0,1:T(8,128)} %copy-done.5) | copy-start | bytes 110596
  77.2 15.2 %copy-start.8 = (f32[1,3072]{0,1:T(8,128)S(1)}, f32[1,3072]{0,1:T(8,128)}, u32[]{:S(2)}) copy-start(f32[1,3072]{0,1:T(8,128)} %copy-done.7) | copy-start | bytes 36868
  77.2 15.2 %copy-start.25 = (f32[1,3072]{0,1:T(8,128)S(1)}, f32[1,3072]{0,1:T(8,128)}, u32[]{:S(2)}) copy-start(f32[1,3072]{0,1:T(8,128)} %get-tuple-element.400) | copy-start | bytes 36868
  77.2 15.2 %copy-start.29 = (f32[1,3072]{0,1:T(8,128)S(1)}, f32[1,3072]{0,1:T(8,128)}, u32[]{:S(2)}) copy-start(f32[1,3072]{0,1:T(8,128)} %get-tuple-element.421) | copy-start | bytes 36868
  111.4 12.5 %copy-start.41 = (f32[3072]{0:T(1024)S(1)}, f32[3072]{0:T(1024)}, u32[]{:S(2)}) copy-start(f32[3072]{0:T(1024)} %get-tuple-element.273) | copy-start | bytes 36868
  111.4 12.5 %copy-start.42 = (f32[3072]{0:T(1024)S(1)}, f32[3072]{0:T(1024)}, u32[]{:S(2)}) copy-start(f32[3072]{0:T(1024)} %get-tuple-element.274) | copy-start | bytes 36868
  111.4 12.5 %copy-start.43 = (f32[3072]{0:T(1024)S(1)}, f32[3072]{0:T(1024)}, u32[]{:S(2)}) copy-start(f32[3072]{0:T(1024)} %get-tuple-element.275) | copy-start | bytes 36868
  111.5 12.5 %copy-start.44 = (f32[3072]{0:T(1024)S(1)}, f32[3072]{0:T(1024)}, u32[]{:S(2)}) copy-start(f32[3072]{0:T(1024)} %get-tuple-element.276) | copy-start | bytes 36868
  111.5 12.5 %copy-start.45 = (f32[3072]{0:T(1024)S(1)}, f32[3072]{0:T(1024)}, u32[]{:S(2)}) copy-start(f32[3072]{0:T(1024)} %get-tuple-element.281) | copy-start | bytes 36868
  111.5 12.5 %copy-start.46 = (f32[3072]{0:T(1024)S(1)}, f32[3072]{0:T(1024)}, u32[]{:S(2)}) copy-start(f32[3072]{0:T(1024)} %get-tuple-element.282) | copy-start | bytes 36868
  124.1 24.5 %copy-start.35 = (f32[4,1,1,3072]{3,2,1,0:T(1,128)S(1)}, f32[4,1,1,3072]{3,2,1,0:T(1,128)}, u32[]{:S(2)}) copy-start(f32[4,1,1,3072]{3,2,1,0:T(1,128)} %param.25) | copy-start | bytes 147460
  141.3 8.8 %collective-permute-start = (f32[39,3]{1,0:T(8,128)S(1)}, f32[39,3]{1,0:T(8,128)S(1)}, u32[]{:S(2)}, u32[]{:S(2)}) collective-permute-start(f32[39,3]{1,0:T(8,128)S(1)} %slice.983), channel_id=1, source_target_pairs={{0,8},{8,16},{16,24},{24,32},{32,40},{40,48},{48,56},{56,64},{64,7... | collective-permute-start | bytes 1412 | tf_op jit(solution)/shard_map/ppermute | solution.py:23
  150.9 20.4 %all-to-all-start = ((f32[8,39,96]{2,1,0:T(8,128)}), f32[8,39,96]{2,1,0:T(8,128)S(1)}, u32[]{:S(2)}, u32[]{:S(2)}) async-start(f32[8,39,96]{2,1,0:T(8,128)} %broadcast_in_dim.45), calls=%async_computation | async-start | bytes 327680 | tf_op jit(solution)/shard_map/all_to_all | solution.py:28
  157.2 476.3 %all-reduce.6.cloned.1.call-start = ((), (), s32[]{:S(2)}) async-start(), calls=%async_computation.1 | async-start | bytes 450560 | tf_op jit(solution)/shard_map/psum | solution.py:50
  171.2 74.3 %copy-start.86 = (pred[3072]{0:T(1024)(128)(4,1)S(1)}, pred[3072]{0:T(1024)(128)(4,1)}, u32[]{:S(2)}) copy-start(pred[3072]{0:T(1024)(128)(4,1)} %get-tuple-element.478) | copy-start | bytes 9220
  171.2 74.3 %copy-start.87 = (pred[3072]{0:T(1024)(128)(4,1)S(1)}, pred[3072]{0:T(1024)(128)(4,1)}, u32[]{:S(2)}) copy-start(pred[3072]{0:T(1024)(128)(4,1)} %get-tuple-element.481) | copy-start | bytes 9220
  171.6 8.5 %collective-permute-start.2 = (f32[36,3]{1,0:T(8,128)S(1)}, f32[36,3]{1,0:T(8,128)S(1)}, u32[]{:S(2)}, u32[]{:S(2)}) collective-permute-start(f32[36,3]{1,0:T(8,128)S(1)} %slice.999), channel_id=1, source_target_pairs={{0,8},{8,16},{16,24},{24,32},{32,40},{40,48},{48,56},{56,64},{64,7... | collective-permute-start | bytes 1304 | tf_op jit(solution)/shard_map/ppermute | solution.py:23
  173.5 5.6 collective-permute-start.1
  175.9 3.9 collective-permute-start.3
  180.6 6.1 collective-permute-start.4
  182.5 4.9 collective-permute-start.5
  188.1 6.1 collective-permute-start.6
  190.0 4.9 collective-permute-start.7
  196.0 5.4 collective-permute-start.8
  337.2 32.4 %copy-start.90 = (f32[1,96]{1,0:T(1,128)S(1)}, f32[1,96]{1,0:T(1,128)}, u32[]{:S(2)}) copy-start(f32[1,96]{1,0:T(1,128)} %get-tuple-element.491) | copy-start | bytes 1156
  337.2 32.4 %copy-start.91 = (f32[1,96]{1,0:T(1,128)S(1)}, f32[1,96]{1,0:T(1,128)}, u32[]{:S(2)}) copy-start(f32[1,96]{1,0:T(1,128)} %get-tuple-element.493) | copy-start | bytes 1156
  641.1 17.1 %copy-start.26 = (f32[6,1,1,3072]{0,3,2,1:T(8,128)S(1)}, f32[6,1,1,3072]{0,3,2,1:T(8,128)}, u32[]{:S(2)}) copy-start(f32[6,1,1,3072]{0,3,2,1:T(8,128)} %copy.795) | copy-start | bytes 221188
  641.2 17.1 %copy-start.88 = (pred[3072]{0:T(1024)(128)(4,1)S(1)}, pred[3072]{0:T(1024)(128)(4,1)}, u32[]{:S(2)}) copy-start(pred[3072]{0:T(1024)(128)(4,1)} %compare_and_fusion.4) | copy-start | bytes 9220
  (71 other events, 329.6 us)
Sparse Core Ops, SparseCore 0:
  369.7 263.6 all-reduce.5
where the time goes:
time: 684 us; the launch traced here: 671 us
  waiting for transfers between devices  269 us (39%)
  local copies, waits for them, and re-layouts  194 us (28%)
  other arithmetic  139 us (20%)
  starting transfers between devices  32.5 us (5%)
  between operations  25.3 us (4%)
  matrix products  12.1 us (2%)
    psum x1, waiting for transfers between devices, packed_total(): running = lax.psum(ravelled, axis)  263 us
    mul x5, other arithmetic, node_features(): weights * vectors[basis_no][first] * vectors[basis_no + offset][second]  54.2 us
    gather x4, local copies, waits for them, and re-layouts, per_device(): picked_nodes = jnp.take(node_values, local_knot + basis_no, axis=1)  43.8 us
    mul x21, local copies, waits for them, and re-layouts, unit_matrix_terms(): weights * rows_part[first] * rows_part[second]  35.3 us
    mul x2, other arithmetic, node_features(): term_list.append(weights * vectors[basis_no][first] * first_res)  22.6 us
    concatenate x1, local copies, waits for them, and re-layouts, packed_total(): jnp.concatenate([a.reshape(-1) for a in arrays])  19.8 us
    mul x2, other arithmetic, rhs_terms(): weights * rows_part[first] * resid_now  15.3 us
    another operation x4, local copies, waits for them, and re-layouts, node_features(): return jnp.stack(term_list)  14.5 us
  transfers between devices with their start and end apart: 11, of which 5 were waited for; matrix products, arithmetic and copies ran while one was open for 3% of the time, Pallas kernels for 0%

commit v1 on v0

v1 whole, which is shorter than its diff:
```python
import jax
import jax.numpy as jnp
from jax import lax
from jax.experimental import pallas as pl
from jax.experimental.pallas import tpu as pltpu
from jax.sharding import PartitionSpec as P

LANES = 128
TILES = 24
KPT = 4
UNITS = 2048
CPAR = 6
GPAR = 4
SPAR = 5
ATT_SWEEPS = 4
ND = 96
HALO = 9
OMEGA = 0.6
RIDGE = 1.0
HI = 8
LO = 256
BASES = (27, 21, 15, 9)
F32 = jnp.float32
BF16 = jnp.bfloat16


def pairs(extent):
    return [(a, b) for a in range(extent) for b in range(a, extent)]


PAIR_AT = {extent: {p: i for i, p in enumerate(pairs(extent))} for extent in (3, 4, 6)}


def entry(values, extent, a, b):
    return values[PAIR_AT[extent][(min(a, b), max(a, b))]]


def factor(values, extent):
    low = [[None] * extent for _ in range(extent)]
    inv = [None] * extent
    for c in range(extent):
        pivot = entry(values, extent, c, c) + RIDGE
        for k in range(c):
            pivot = pivot - low[c][k] * low[c][k]
        low[c][c] = jnp.sqrt(pivot)
        inv[c] = 1.0 / low[c][c]
        for r in range(c + 1, extent):
            value = entry(values, extent, r, c)
            for k in range(c):
                value = value - low[r][k] * low[c][k]
            low[r][c] = value * inv[c]
    return low, inv


def forward(low, inv, vector):
    out = []
    for r in range(len(vector)):
        value = vector[r]
        for k in range(r):
            value = value - low[r][k] * out[k]
        out.append(value * inv[r])
    return out


def backward(low, inv, vector):
    extent = len(vector)
    out = [None] * extent
    for r in reversed(range(extent)):
        value = vector[r]
        for k in range(r + 1, extent):
            value = value - low[k][r] * out[k]
        out[r] = value * inv[r]
    return out


def spline(u):
    v = 1.0 - u
    s = u * u
    c = s * u
    sixth = 1.0 / 6.0
    return [
        v * v * v * sixth,
        (3.0 * c - 6.0 * s + 4.0) * sixth,
        (-3.0 * c + 3.0 * s + 3.0 * u + 1.0) * sixth,
        c * sixth,
    ]


def halves(x):
    top = x.astype(BF16).astype(F32)
    return top, x - top


def dot_nt(a, b):
    return lax.dot_general(a, b, (((1,), (1,)), ((), ())), preferred_element_type=F32)


def attitude_kernel(res, w, sp, si, sd, ap, ph, kn, first_out, att_out, feat, lhs, hot, acc):
    index = si[...]
    row_id = index >> 7
    lane_id = index & (LANES - 1)
    picked = [jnp.zeros((TILES, LANES), F32) for _ in range(SPAR)]
    for h in range(sd.shape[1]):
        mine = row_id == h
        for c in range(SPAR):
            row = jnp.broadcast_to(sd[c, h : h + 1, :], (TILES, LANES))
            picked[c] = jnp.where(mine, jnp.take_along_axis(row, lane_id, axis=1), picked[c])
    total = sp[0] * picked[0]
    for c in range(1, SPAR):
        total = total + sp[c] * picked[c]
    first = res[...] - total
    first_out[...] = first
    basis = spline(ph[...])
    weight = w[...]
    att = [ap[a] for a in range(3)]
    outer = [weight * att[a] * att[b] for a, b in pairs(3)]
    right = [weight * att[a] * first for a in range(3)]
    at = 0
    for i in range(4):
        for value in right:
            feat[pl.ds(at * TILES, TILES), :] = basis[i] * value
            at += 1
        for d in range(4 - i):
            both = basis[i] * basis[i + d]
            for value in outer:
                feat[pl.ds(at * TILES, TILES), :] = both * value
                at += 1
    count = at
    padded = lhs.shape[0] // 2
    node = lax.broadcasted_iota(jnp.int32, (LANES, LANES), 0)
    for t in range(TILES):
        cols = slice(t * LANES, (t + 1) * LANES)
        top, low = halves(feat[pl.ds(t, count, stride=TILES), :])
        lhs[0:count, cols] = top.astype(BF16)
        lhs[padded : padded + count, cols] = low.astype(BF16)
        slot = (kn[t : t + 1, :] & (KPT - 1)) + (KPT * t + HALO)
        hot[:, cols] = jnp.where(node == slot, 1.0, 0.0).astype(BF16)
    both = dot_nt(lhs[...], hot[...])
    acc[...] = both[:padded] + both[padded:]
    att_out[...] = jnp.zeros_like(att_out)
    at = 0
    for i, rows in enumerate(BASES):
        value = acc[at : at + rows, :]
        if i:
            value = pltpu.roll(value, i, 1)
        att_out[0:rows, :] = att_out[0:rows, :] + value
        at += rows


def unit_hot(unit, hot):
    lo_id = lax.broadcasted_iota(jnp.int32, (LO, LANES), 0)
    for t in range(TILES):
        cols = slice(t * LANES, (t + 1) * LANES)
        lo = unit[t : t + 1, :] & (LO - 1)
        hot[:, cols] = jnp.where(lo_id == lo, 1.0, 0.0).astype(BF16)


def spread(unit, feats, parts, base, top_to, low_to):
    for f, value in enumerate(feats):
        top, low = halves(value)
        parts[0, pl.ds(f * TILES, TILES), :] = top
        parts[1, pl.ds(f * TILES, TILES), :] = low
    hi_id = lax.broadcasted_iota(jnp.int32, (HI, LANES), 0)
    zero = jnp.zeros((HI, LANES), F32)
    for t in range(TILES):
        cols = slice(t * LANES, (t + 1) * LANES)
        mine = hi_id == (unit[t : t + 1, :] >> 8)
        for part, to in ((0, top_to), (1, low_to)):
            for f in range(0, len(feats), 2):
                rows = []
                for g in (f, f + 1):
                    if g < len(feats):
                        row = parts[part, g * TILES + t : g * TILES + t + 1, :]
                        rows.append(jnp.where(mine, jnp.broadcast_to(row, (HI, LANES)), 0.0))
                    else:
                        rows.append(zero)
                to[base + f * HI : base + (f + 2) * HI, cols] = jnp.concatenate(rows, axis=0).astype(BF16)


def totals_row(values, first_lane):
    lane = lax.broadcasted_iota(jnp.int32, (1, LANES), 1)
    row = jnp.zeros((1, LANES), F32)
    for k, value in enumerate(values):
        folded = value[0:8] + value[8:16] + value[16:24]
        total = jnp.sum(jnp.sum(folded, axis=1, keepdims=True), axis=0, keepdims=True)
        row = jnp.where(lane == first_lane + k, total, row)
    return row


N_C = CPAR * (CPAR + 1) // 2
N_G = GPAR * (GPAR + 1) // 2
E_COL = N_C * HI - LANES
G_COL = E_COL + CPAR * HI
H_COL = G_COL + N_G


def matrix_kernel(w, cp, ci, gp, left_out, right_out, hot_out, parts, top, low):
    weight = w[...]
    calib = [cp[a] for a in range(CPAR)]
    weighted = [weight * c for c in calib]
    feats = [weighted[a] * calib[b] for a, b in pairs(CPAR)]
    used = (N_C + 1) // 2 * 2 * HI
    top[used:, :] = jnp.zeros((2 * LANES - used, top.shape[1]), BF16)
    low[used:, :] = jnp.zeros((2 * LANES - used, top.shape[1]), BF16)
    spread(ci, feats, parts, 0, top, low)
    unit_hot(ci, hot_out)
    hot = hot_out[...]
    both = dot_nt(hot, top[...]) + dot_nt(hot, low[...])
    glob = [gp[a] for a in range(GPAR)]
    sums = totals_row([weight * glob[a] * glob[b] for a, b in pairs(GPAR)], G_COL)
    left_out[...] = both[:, :LANES]
    right_out[...] = both[:, LANES:] + sums


def sweep_kernel(
    own, left, right, kn, first_in, ph, ap, w, cp, ci, gp, hot, zl, zr, second_out, step_out, z_out, ext, parts, top, low
):
    lane = lax.broadcasted_iota(jnp.int32, (32, LANES), 1)
    summed = own[...]
    summed = summed + jnp.where(lane < 12, pltpu.roll(left[...], 32, 1), 0.0)
    summed = summed + jnp.where((lane >= 105) & (lane < 117), pltpu.roll(right[...], 96, 1), 0.0)
    ext[...] = summed
    row = [ext[r : r + 1, :] for r in range(27)]
    base = jnp.broadcast_to(kn[0:1, 0:1] & ~(KPT - 1), (1, LANES))
    node = base + lax.broadcasted_iota(jnp.int32, (1, LANES), 1) - HALO
    exists = (node >= 0) & (node < NODES)
    rhs = row[0:3]
    band = [row[3 + 6 * d : 9 + 6 * d] for d in range(4)]
    low3, inv3 = factor(band[0], 3)

    def precondition(vector):
        return [OMEGA * v for v in backward(low3, inv3, forward(low3, inv3, vector))]

    def times(values, x, a):
        out = entry(values, 3, a, 0) * x[0]
        out = out + entry(values, 3, a, 1) * x[1]
        return out + entry(values, 3, a, 2) * x[2]

    def kept(values):
        return [jnp.where(exists, v, 0.0) for v in values]

    x = kept(precondition(rhs))
    for _ in range(1, ATT_SWEEPS):
        rest = [rhs[a] - x[a] - times(band[0], x, a) for a in range(3)]
        for d in range(1, 4):
            ahead = [pltpu.roll(v, LANES - d, 1) for v in x]
            for a in range(3):
                rest[a] = rest[a] - times(band[d], ahead, a)
                rest[a] = rest[a] - pltpu.roll(times(band[d], x, a), d, 1)
        step = precondition(rest)
        x = kept([x[a] + step[a] for a in range(3)])
    for c in range(3):
        value = low3[c][c] * x[c]
        for k in range(c + 1, 3):
            value = value + low3[k][c] * x[k]
        step_out[c : c + 1, :] = pltpu.roll(value, LANES - HALO, 1)[:, :ND]
    tile = lax.broadcasted_iota(jnp.int32, (TILES, LANES), 0)
    local = (kn[...] & (KPT - 1)) + KPT * tile + HALO
    basis = spline(ph[...])
    att = [ap[a] for a in range(3)]
    spread_x = [jnp.broadcast_to(v, (TILES, LANES)) for v in x]
    second = first_in[...]
    for i in range(4):
        dot = att[0] * jnp.take_along_axis(spread_x[0], local + i, axis=1)
        for a in range(1, 3):
            dot = dot + att[a] * jnp.take_along_axis(spread_x[a], local + i, axis=1)
        second = second - basis[i] * dot
    second_out[...] = second
    push = w[...] * second
    feats = [push * cp[a] for a in range(CPAR)]
    top[...] = jnp.zeros_like(top)
    low[...] = jnp.zeros_like(low)
    spread(ci, feats, parts, E_COL, top, low)
    both = dot_nt(hot[...], top[...]) + dot_nt(hot[...], low[...])
    sums = totals_row([push * gp[a] for a in range(GPAR)], H_COL)
    z_out[pl.ds(0, LO, stride=2), :] = zl[...]
    z_out[pl.ds(1, LO, stride=2), :] = zr[...] + both + sums


def at_lane(row, start):
    return pltpu.roll(row, (LANES - start) % LANES, 1) if start else row


def solve_kernel(z, row_out, glob_out, fold):
    parts = [z[8 * k : 8 * k + 8, :] for k in range(z.shape[0] // 8)]
    while len(parts) > 1:
        parts = [a + b for a, b in zip(parts[::2], parts[1::2])]
    fold[...] = parts[0]
    left = fold[0:1, :] + fold[2:3, :] + fold[4:5, :] + fold[6:7, :]
    right = fold[1:2, :] + fold[3:4, :] + fold[5:6, :] + fold[7:8, :]
    columns = [at_lane(left if f < 16 else right, f * HI % LANES) for f in range(N_C + CPAR)]
    low6, inv6 = factor(columns[:N_C], CPAR)
    white = forward(low6, inv6, columns[N_C:])
    solved = backward(low6, inv6, white)
    lane = lax.broadcasted_iota(jnp.int32, (1, LANES), 1)
    row = jnp.zeros((1, LANES), F32)
    for j, value in enumerate(white + solved):
        moved = pltpu.roll(value, j * HI, 1) if j else value
        row = jnp.where((lane >= j * HI) & (lane < (j + 1) * HI), moved, row)
    row_out[...] = jnp.broadcast_to(row, row_out.shape)
    glob = [at_lane(right, G_COL + k) for k in range(N_G + GPAR)]
    low4, inv4 = factor(glob[:N_G], GPAR)
    white4 = forward(low4, inv4, glob[N_G:])
    solved4 = backward(low4, inv4, white4)
    for k, value in enumerate(white4 + solved4):
        glob_out[k : k + 1, :] = value


def final_kernel(table, second, cp, ci, gp, glob, res_out, calib_out, rows):
    rows[:, 0:LANES] = jnp.transpose(table[0:LANES, :])
    rows[:, LANES:] = jnp.transpose(table[LANES:, :])
    for j in range(CPAR):
        for h in range(HI):
            calib_out[j : j + 1, h * LO : (h + 1) * LO] = rows[j * HI + h : j * HI + h + 1, :]
    unit = ci[...]
    row_id = unit >> 7
    lane_id = unit & (LANES - 1)
    picked = [jnp.zeros((TILES, LANES), F32) for _ in range(CPAR)]
    for h in range(2 * HI):
        mine = row_id == h
        half = (h & 1) * LANES
        for c in range(CPAR):
            at = (CPAR + c) * HI + (h >> 1)
            row = jnp.broadcast_to(rows[at : at + 1, half : half + LANES], (TILES, LANES))
            picked[c] = jnp.where(mine, jnp.take_along_axis(row, lane_id, axis=1), picked[c])
    total = cp[0] * picked[0]
    for c in range(1, CPAR):
        total = total + cp[c] * picked[c]
    out = second[...] - total
    shift = gp[0] * glob[GPAR : GPAR + 1, 0:1]
    for a in range(1, GPAR):
        shift = shift + gp[a] * glob[GPAR + a : GPAR + a + 1, 0:1]
    res_out[...] = out - shift


NODES = 3072


def shifted(x, by):
    count = lax.axis_size("tm")
    return lax.ppermute(x, "tm", [(i, i + by) for i in range(count) if 0 <= i + by < count])


def call(kernel, outs, scratch, *args, flops=0):
    out_shape = [jax.ShapeDtypeStruct(s, d) for s, d in outs]
    return pl.pallas_call(
        kernel,
        out_shape=out_shape,
        scratch_shapes=[pltpu.VMEM(s, d) for s, d in scratch],
        cost_estimate=pl.CostEstimate(flops=flops, transcendentals=0, bytes_accessed=1 << 20),
    )(*args)


def per_device(res, w, sp, si, sd, ap, ph, kn, cp, ci, gp):
    tiles = (TILES, LANES)
    rows = TILES * LANES
    res, w, si, ph, kn, ci = (x.reshape(tiles) for x in (res, w, si, ph, kn, ci))
    sp, ap, cp, gp = (x.reshape(x.shape[0], *tiles) for x in (sp, ap, cp, gp))
    sd = sd.reshape(SPAR, -1, LANES)
    feat_rows = sum(BASES)
    padded = -(-feat_rows // 16) * 16
    first, att = call(
        attitude_kernel,
        [(tiles, F32), ((32, LANES), F32)],
        [((feat_rows * TILES, LANES), F32), ((2 * padded, rows), BF16), ((LANES, rows), BF16), ((padded, LANES), F32)],
        res, w, sp, si, sd, ap, ph, kn, flops=1 << 24,
    )
    groups = lax.axis_size("grp")
    copies = jnp.broadcast_to(att, (groups, *att.shape))
    gathered = lax.all_to_all(copies, "grp", split_axis=0, concat_axis=0, tiled=True)
    zl, zr, hot = call(
        matrix_kernel,
        [((LO, LANES), F32), ((LO, LANES), F32), ((LO, rows), BF16)],
        [((2, N_C * TILES, LANES), F32), ((2 * LANES, rows), BF16), ((2 * LANES, rows), BF16)],
        w, cp, ci, gp, flops=1 << 25,
    )
    own = gathered.sum(axis=0)
    left = shifted(own, 1)
    right = shifted(own, -1)
    second, step, z = call(
        sweep_kernel,
        [(tiles, F32), ((3, ND), F32), ((2 * LO, LANES), F32)],
        [((32, LANES), F32), ((2, CPAR * TILES, LANES), F32), ((LANES, rows), BF16), ((LANES, rows), BF16)],
        own, left, right, kn, first, ph, ap, w, cp, ci, gp, hot, zl, zr, flops=1 << 24,
    )
    both = ("tm", "grp")
    z = lax.all_to_all(z.reshape(LO, 2, LANES), both, split_axis=0, concat_axis=0, tiled=True)
    copies, glob = call(
        solve_kernel,
        [((LO, LANES), F32), ((2 * GPAR, LANES), F32)],
        [((8, LANES), F32)],
        z.reshape(2 * LO, LANES),
    )
    table = lax.all_to_all(copies.reshape(LO, 1, LANES), both, split_axis=0, concat_axis=0, tiled=True)
    out, calib = call(
        final_kernel,
        [(tiles, F32), ((CPAR, UNITS), F32)],
        [((LANES, LO), F32)],
        table.reshape(LO, LANES), second, cp, ci, gp, glob,
    )
    return out.reshape(1, 1, rows), step, calib, glob[:GPAR, 0]


def solution(mesh):
    return jax.shard_map(
        per_device,
        mesh=mesh,
        in_specs=(
            P("tm", "grp", None),
            P("tm", "grp", None),
            P(None, "tm", "grp", None),
            P("tm", "grp", None),
            P(None, "tm", None),
            P(None, "tm", "grp", None),
            P("tm", "grp", None),
            P("tm", "grp", None),
            P(None, "tm", "grp", None),
            P("tm", "grp", None),
            P(None, "tm", "grp", None),
        ),
        out_specs=(P("tm", "grp", None), P(None, "tm"), P(), P()),
        check_vma=False,
    )
```

time: 684 us -> 84.1 us (0.12); the launches traced: 671 us -> 83.6 us
  waiting for transfers between devices: 269 us -> 11.7 us
  local copies, waits for them, and re-layouts: 194 us -> 3.27 us
  other arithmetic: 139 us -> 0.01 us
  blocking collectives: 0 us -> 41.7 us
  between operations: 25.3 us -> 0.69 us
  starting transfers between devices: 32.5 us -> 11.2 us
  Pallas kernels: 0 us -> 14.9 us
  matrix products: 12.1 us -> 0 us
    psum x1 -> x0, waiting for transfers between devices: 263 us -> none  [packed_total(): running = lax.psum(ravelled, axis)]
    mul x13 -> x0, other arithmetic: 107 us -> none  [the longest x5 54.2 us: node_features(): weights * vectors[basis_no][first] * vectors[basis_no + offset][second]]
    gather x6 -> x0, local copies, waits for them, and re-layouts: 64.4 us -> none  [the longest x4 43.8 us: per_device(): picked_nodes = jnp.take(node_values, local_knot + basis_no, axis=1)]
    mul x27 -> x0, local copies, waits for them, and re-layouts: 47.9 us -> none  [the longest x21 35.3 us: unit_matrix_terms(): weights * rows_part[first] * rows_part[second]]
    all_to_all x0 -> x2, blocking collectives: none -> 41.7 us  [the longest x1 27.4 us: per_device(): lax.all_to_all(z.reshape(LO, 2, LANES), both, split_axis=0, concat_axis=0...]
    concatenate x5 -> x0, local copies, waits for them, and re-layouts: 21.8 us -> none  [the longest x1 19.8 us: packed_total(): jnp.concatenate([a.reshape(-1) for a in arrays])]
    ppermute x9 -> x2, starting transfers between devices: 26.1 us -> 6.13 us  [shifted(): lax.ppermute(x, 'tm', [(i, i + by) for i in range(count) if 0 <= i + by <...]
    reduce_sum x28 -> x1, other arithmetic: 16.6 us -> 0.01 us  [per_device(): own = gathered.sum(axis=0)]
  transfers between devices with their start and end apart: 11 -> 3, of which waited for: 5 -> 1; matrix products, arithmetic and copies ran while one was open for 3% -> 2% of each run, Pallas kernels for 0% -> 4%
where the time goes in v1:
time: 84.1 us; the launch traced here: 83.6 us
  blocking collectives  41.7 us (50%)
  Pallas kernels  14.9 us (18%)
  waiting for transfers between devices  11.7 us (14%)
  starting transfers between devices  11.2 us (13%)
  local copies, waits for them, and re-layouts  3.27 us (4%)
    all_to_all x1, blocking collectives, per_device(): lax.all_to_all(z.reshape(LO, 2, LANES), both, split_axis=0, concat_axis=0...  27.4 us
    pallas_call x5, Pallas kernels, call(): pl.pallas_call(kernel, out_shape=out_shape, scratch_shapes=[pltpu.VMEM(s,...  14.9 us
    all_to_all x1, blocking collectives, per_device(): lax.all_to_all(copies, 'grp', split_axis=0, concat_axis=0, tiled=True)  14.3 us
    all_to_all x1, waiting for transfers between devices, per_device(): lax.all_to_all(copies.reshape(LO, 1, LANES), both, split_axis=0, concat_a...  11.7 us
    ppermute x2, starting transfers between devices, shifted(): lax.ppermute(x, 'tm', [(i, i + by) for i in range(count) if 0 <= i + by <...  6.13 us
    all_to_all x1, starting transfers between devices, per_device(): lax.all_to_all(copies.reshape(LO, 1, LANES), both, split_axis=0, concat_a...  5.1 us
  transfers between devices with their start and end apart: 3, of which 1 were waited for; matrix products, arithmetic and copies ran while one was open for 2% of the time, Pallas kernels for 4%

profile of v1, /device:TPU:1, one launch (start us, length us, event | category | flops | bytes accessed | tf_op | source)
XLA Modules:
  0.0 83.6 jit_solution(12969630669421227295)
XLA Ops:
  0.6 3.4 %shard_map.138 = (f32[24,128]{1,0:T(8,128)}, f32[32,128]{1,0:T(8,128)}) custom-call(f32[24,128]{1,0:T(8,128)} %bitcast.42, f32[24,128]{1,0:T(8,128)} %bitcast.33, f32[5,24,128]{2,1,0:T(8,128)} %bitcast.37, s32[24,128]{1,0:T(8,128)} %bitcast.43, f32[5,32,128]{2,1,0:T(8,128)} %bitcast.36, f32[3,24,128]{2,1,0:T(8,128)} %bitcast.27, f32[24,128]{1,0:T(8,128)} %bitcast.38, ...), custom_call_target="tpu_custom_call" | custom-call | flops 16777216 | bytes 1048576 | tf_op jit(solution)/shard_map/pallas_call | solution.py:346
  4.0 0.7 broadcast_in_dim.3
  4.8 14.3 %all_to_all.15 = f32[8,32,128]{2,1,0:T(8,128)S(1)} all-to-all(f32[8,32,128]{2,1,0:T(8,128)S(1)} %broadcast_in_dim.3), channel_id=1, replica_groups=mesh['tm'=32,'grp'=8] {'grp'}, dimensions={0} | all-to-all | bytes 262144 | tf_op jit(solution)/shard_map/all_to_all | solution.py:370
  19.1 0.0 copy-start.1
  19.1 4.0 %collective-permute-start.1 = (f32[32,128]{1,0:T(8,128)S(1)}, f32[32,128]{1,0:T(8,128)S(1)}, u32[]{:S(2)}, u32[]{:S(2)}) collective-permute-start(f32[32,128]{1,0:T(8,128)S(1)} %reduce_sum.9.own), channel_id=1, source_target_pairs={{8,0},{16,8},{24,16},{32,24},{40,32},{48,40},{56,48},{64,56},{72,6... | collective-permute-start | bytes 49160 | tf_op jit(solution)/shard_map/ppermute | solution.py:341
  23.1 2.1 %collective-permute-start = (f32[32,128]{1,0:T(8,128)S(1)}, f32[32,128]{1,0:T(8,128)S(1)}, u32[]{:S(2)}, u32[]{:S(2)}) collective-permute-start(f32[32,128]{1,0:T(8,128)S(1)} %reduce_sum.9.own), channel_id=1, source_target_pairs={{0,8},{8,16},{16,24},{24,32},{32,40},{40,48},{48,56},{56,64},{64,7... | collective-permute-start | bytes 49160 | tf_op jit(solution)/shard_map/ppermute | solution.py:341
  25.2 3.3 %shard_map.139 = (f32[256,128]{1,0:T(8,128)}, f32[256,128]{1,0:T(8,128)}, bf16[256,3072]{1,0:T(8,128)(2,1)}) custom-call(f32[24,128]{1,0:T(8,128)} %bitcast.34, f32[6,24,128]{2,1,0:T(8,128)} %bitcast.19, s32[24,128]{1,0:T(8,128)} %bitcast.30, f32[4,24,128]{2,1,0:T(8,128)} %bitcast.23), custom_call_target="tpu_custom_call" | custom-call | flops 33554432 | bytes 1048576 | tf_op jit(solution)/shard_map/pallas_call | solution.py:346
  28.6 0.0 collective-permute-done.1.right
  28.6 0.0 copy-start.2
  28.6 0.0 collective-permute-done.left
  28.6 0.0 copy-start.3
  28.6 0.0 copy-done.1
  28.6 0.6 copy-done.2
  29.2 0.0 copy-done.3
  29.2 3.8 %shard_map.140 = (f32[24,128]{1,0:T(8,128)}, f32[3,96]{1,0:T(4,128)}, f32[512,128]{1,0:T(8,128)}) custom-call(f32[32,128]{1,0:T(8,128)} %copy-done.1, f32[32,128]{1,0:T(8,128)} %copy-done.3, f32[32,128]{1,0:T(8,128)} %copy-done.2, s32[24,128]{1,0:T(8,128)} %bitcast.41, f32[24,128]{1,0:T(8,128)} %get-tuple-element.17.first_in, f32[24,128]{1,0:T(8,128)} %bitcast.39, ...), custom_call_target="tpu_custom_call" | custom-call | flops 16777216 | bytes 1048576 | tf_op jit(solution)/shard_map/pallas_call | solution.py:346
  33.0 27.4 %all_to_all.16 = f32[256,2,128]{2,1,0:T(2,128)} all-to-all(f32[256,2,128]{2,1,0:T(2,128)} %bitcast.26), channel_id=1, replica_groups=mesh['tm'=32,'grp'=8] {'tm','grp'}, dimensions={0} | all-to-all | bytes 524288 | tf_op jit(solution)/shard_map/all_to_all | solution.py:387
  60.4 1.9 %shard_map.141 = (f32[256,128]{1,0:T(8,128)}, f32[8,128]{1,0:T(8,128)}) custom-call(f32[512,128]{1,0:T(8,128)} %bitcast.18), custom_call_target="tpu_custom_call" | custom-call | bytes 1048576 | tf_op jit(solution)/shard_map/pallas_call | solution.py:346
  62.3 5.1 %all-to-all-start.2 = ((f32[256,1,128]{2,1,0:T(1,128)}), f32[256,1,128]{2,1,0:T(1,128)S(1)}, u32[]{:S(2)}, u32[]{:S(2)}) async-start(f32[256,1,128]{2,1,0:T(1,128)} %bitcast.29), calls=%async_computation.2 | async-start | bytes 262144 | tf_op jit(solution)/shard_map/all_to_all | solution.py:394
  67.4 1.3 %slice_reduce_fusion = f32[4]{0:T(128)} fusion(f32[8,128]{1,0:T(8,128)} %get-tuple-element.24.glob), kind=kLoop, calls=%fused_computation | loop fusion | bytes 32 | tf_op jit(solution)/shard_map/slice | solution.py:401
  68.7 11.7 %all-to-all-done.2 = f32[256,1,128]{2,1,0:T(1,128)S(1)} async-done(((f32[256,1,128]{2,1,0:T(1,128)}), f32[256,1,128]{2,1,0:T(1,128)S(1)}, u32[]{:S(2)}, u32[]{:S(2)}) %all-to-all-start.2) | async-done | bytes 131104 | tf_op jit(solution)/shard_map/all_to_all | solution.py:394
  80.5 0.0 copy-start
  80.5 0.7 copy-done
  81.1 2.5 %shard_map.142 = (f32[24,128]{1,0:T(8,128)}, f32[6,2048]{1,0:T(8,128)}) custom-call(f32[256,128]{1,0:T(8,128)} %bitcast.22, f32[24,128]{1,0:T(8,128)} %get-tuple-element.23.second, f32[6,24,128]{2,1,0:T(8,128)} %bitcast.21, s32[24,128]{1,0:T(8,128)} %bitcast.32, f32[4,24,128]{2,1,0:T(8,128)} %bitcast.25, f32[8,128]{1,0:T(8,128)} %get-tuple-element.24.glob), custom_call_target="tpu_custom_call" | custom-call | bytes 1048576 | tf_op jit(solution)/shard_map/pallas_call | solution.py:346
  (1 shorter events, 0.0 us)
Async XLA Ops:
  19.1 9.5 %copy-start.1 = (f32[32,128]{1,0:T(8,128)}, f32[32,128]{1,0:T(8,128)S(1)}, u32[]{:S(2)}) copy-start(f32[32,128]{1,0:T(8,128)S(1)} %reduce_sum.9.own) | copy-start | bytes 49156
  19.1 9.5 %collective-permute-start.1 = (f32[32,128]{1,0:T(8,128)S(1)}, f32[32,128]{1,0:T(8,128)S(1)}, u32[]{:S(2)}, u32[]{:S(2)}) collective-permute-start(f32[32,128]{1,0:T(8,128)S(1)} %reduce_sum.9.own), channel_id=1, source_target_pairs={{8,0},{16,8},{24,16},{32,24},{40,32},{48,40},{56,48},{64,56},{72,6... | collective-permute-start | bytes 49160 | tf_op jit(solution)/shard_map/ppermute | solution.py:341
  23.1 5.5 %collective-permute-start = (f32[32,128]{1,0:T(8,128)S(1)}, f32[32,128]{1,0:T(8,128)S(1)}, u32[]{:S(2)}, u32[]{:S(2)}) collective-permute-start(f32[32,128]{1,0:T(8,128)S(1)} %reduce_sum.9.own), channel_id=1, source_target_pairs={{0,8},{8,16},{16,24},{24,32},{32,40},{40,48},{48,56},{56,64},{64,7... | collective-permute-start | bytes 49160 | tf_op jit(solution)/shard_map/ppermute | solution.py:341
  28.6 0.6 copy-start.2
  28.6 0.6 copy-start.3
  62.3 18.2 %all-to-all-start.2 = ((f32[256,1,128]{2,1,0:T(1,128)}), f32[256,1,128]{2,1,0:T(1,128)S(1)}, u32[]{:S(2)}, u32[]{:S(2)}) async-start(f32[256,1,128]{2,1,0:T(1,128)} %bitcast.29), calls=%async_computation.2 | async-start | bytes 262144 | tf_op jit(solution)/shard_map/all_to_all | solution.py:394
  80.5 0.7 copy-start

commit v2 on v1

--- a/solution.py
+++ b/solution.py
@@ -19,7 +19,8 @@
 RIDGE = 1.0
 HI = 8
 LO = 256
-BASES = (27, 21, 15, 9)
+CHUNK = 8
+BAND = 24
 F32 = jnp.float32
 BF16 = jnp.bfloat16
 
@@ -95,56 +96,86 @@
     return lax.dot_general(a, b, (((1,), (1,)), ((), ())), preferred_element_type=F32)
 
 
-def attitude_kernel(res, w, sp, si, sd, ap, ph, kn, first_out, att_out, feat, lhs, hot, acc):
-    index = si[...]
-    row_id = index >> 7
-    lane_id = index & (LANES - 1)
-    picked = [jnp.zeros((TILES, LANES), F32) for _ in range(SPAR)]
-    for h in range(sd.shape[1]):
-        mine = row_id == h
-        for c in range(SPAR):
-            row = jnp.broadcast_to(sd[c, h : h + 1, :], (TILES, LANES))
-            picked[c] = jnp.where(mine, jnp.take_along_axis(row, lane_id, axis=1), picked[c])
-    total = sp[0] * picked[0]
-    for c in range(1, SPAR):
-        total = total + sp[c] * picked[c]
-    first = res[...] - total
-    first_out[...] = first
+def attitude_kernel(*refs):
+    far, refs = refs[:11], refs[11:]
+    (first_out, att_out), near, refs = refs[:2], refs[2:9], refs[9:]
+    near, refs = (*near, *refs[:4]), refs[4:]
+    feat, lhs, rhs_feat, rhs, hot, acc, shut, sems = refs
+    loads = [pltpu.make_async_copy(a, b, sems.at[i]) for i, (a, b) in enumerate(zip(far, near))]
+    for i in (10, 9, 0, 1, 2, 3, 8, 7, 4, 5, 6):
+        loads[i].start()
+    w, ap, ph, kn, cp, ci, gp, res, sp, si, sd = near
+    for i in (10, 9, 0, 1, 2, 3, 8, 7):
+        loads[i].wait()
     basis = spline(ph[...])
     weight = w[...]
     att = [ap[a] for a in range(3)]
     outer = [weight * att[a] * att[b] for a, b in pairs(3)]
-    right = [weight * att[a] * first for a in range(3)]
     at = 0
     for i in range(4):
-        for value in right:
-            feat[pl.ds(at * TILES, TILES), :] = basis[i] * value
-            at += 1
         for d in range(4 - i):
             both = basis[i] * basis[i + d]
             for value in outer:
                 feat[pl.ds(at * TILES, TILES), :] = both * value
                 at += 1
     count = at
-    padded = lhs.shape[0] // 2
     node = lax.broadcasted_iota(jnp.int32, (LANES, LANES), 0)
+    index = si[...]
+    row_id = index >> 7
+    lane_id = index & (LANES - 1)
+    picked = [jnp.zeros((TILES, LANES), F32) for _ in range(SPAR)]
+    half = lhs.shape[0] // 2
+    band = None
+    steps = TILES // CHUNK
+    for s in range(steps):
+        for t in range(s * CHUNK, (s + 1) * CHUNK):
+            cols = slice(t * LANES, (t + 1) * LANES)
+            top, low = halves(feat[pl.ds(t, count, stride=TILES), :])
+            lhs[0:count, cols] = top.astype(BF16)
+            lhs[half : half + count, cols] = low.astype(BF16)
+            slot = (kn[t : t + 1, :] & (KPT - 1)) + (KPT * t + HALO)
+            hot[:, cols] = jnp.where(node == slot, 1.0, 0.0).astype(BF16)
+        cols = slice(s * CHUNK * LANES, (s + 1) * CHUNK * LANES)
+        part = dot_nt(lhs[:, cols], hot[:, cols])
+        band = part if band is None else band + part
+        for h in range(s * sd.shape[1] // steps, (s + 1) * sd.shape[1] // steps):
+            mine = row_id == h
+            for c in range(SPAR):
+                row = jnp.broadcast_to(sd[c, h : h + 1, :], (TILES, LANES))
+                picked[c] = jnp.where(mine, jnp.take_along_axis(row, lane_id, axis=1), picked[c])
+    acc[...] = band[:half] + band[half:]
+    total = sp[0] * picked[0]
+    for c in range(1, SPAR):
+        total = total + sp[c] * picked[c]
+    first = res[...] - total
+    first_out[...] = first
+    at = 0
+    for i in range(4):
+        for a in range(3):
+            rhs_feat[pl.ds(at * TILES, TILES), :] = basis[i] * (weight * att[a] * first)
+            at += 1
     for t in range(TILES):
         cols = slice(t * LANES, (t + 1) * LANES)
-        top, low = halves(feat[pl.ds(t, count, stride=TILES), :])
-        lhs[0:count, cols] = top.astype(BF16)
-        lhs[padded : padded + count, cols] = low.astype(BF16)
-        slot = (kn[t : t + 1, :] & (KPT - 1)) + (KPT * t + HALO)
-        hot[:, cols] = jnp.where(node == slot, 1.0, 0.0).astype(BF16)
-    both = dot_nt(lhs[...], hot[...])
-    acc[...] = both[:padded] + both[padded:]
-    att_out[...] = jnp.zeros_like(att_out)
+        top, low = halves(rhs_feat[pl.ds(t, at, stride=TILES), :])
+        rhs[0:at, cols] = top.astype(BF16)
+        rhs[16 : 16 + at, cols] = low.astype(BF16)
+    both = dot_nt(rhs[...], hot[...])
+    both = both[:16] + both[16:]
+    shut[...] = jnp.zeros_like(shut)
     at = 0
-    for i, rows in enumerate(BASES):
+    side = both[0:3]
+    for i in range(4):
+        rows = 6 * (4 - i)
         value = acc[at : at + rows, :]
         if i:
             value = pltpu.roll(value, i, 1)
-        att_out[0:rows, :] = att_out[0:rows, :] + value
+            side = side + pltpu.roll(both[3 * i : 3 * i + 3, :], i, 1)
+        shut[0:rows, :] = shut[0:rows, :] + value
         at += rows
+    shut[BAND : BAND + 3, :] = side
+    att_out[...] = jnp.broadcast_to(shut[...][None], att_out.shape)
+    for i in (4, 5, 6):
+        loads[i].wait()
 
 
 def unit_hot(unit, hot):
@@ -155,7 +186,7 @@
         hot[:, cols] = jnp.where(lo_id == lo, 1.0, 0.0).astype(BF16)
 
 
-def spread(unit, feats, parts, base, top_to, low_to):
+def spread(unit, feats, parts, top_to, low_to):
     for f, value in enumerate(feats):
         top, low = halves(value)
         parts[0, pl.ds(f * TILES, TILES), :] = top
@@ -165,7 +196,7 @@
     for t in range(TILES):
         cols = slice(t * LANES, (t + 1) * LANES)
         mine = hi_id == (unit[t : t + 1, :] >> 8)
-        for part, to in ((0, top_to), (1, low_to)):
+        for part, (to, base) in ((0, top_to), (1, low_to)):
             for f in range(0, len(feats), 2):
                 rows = []
                 for g in (f, f + 1):
@@ -174,7 +205,8 @@
                         rows.append(jnp.where(mine, jnp.broadcast_to(row, (HI, LANES)), 0.0))
                     else:
                         rows.append(zero)
-                to[base + f * HI : base + (f + 2) * HI, cols] = jnp.concatenate(rows, axis=0).astype(BF16)
+                at = (base + f * HI) % to.shape[0]
+                to[at : at + 2 * HI, cols] = jnp.concatenate(rows, axis=0).astype(BF16)
 
 
 def totals_row(values, first_lane):
@@ -189,7 +221,7 @@
 
 N_C = CPAR * (CPAR + 1) // 2
 N_G = GPAR * (GPAR + 1) // 2
-E_COL = N_C * HI - LANES
+E_COL = (N_C + 1) // 2 * 2 * HI - LANES
 G_COL = E_COL + CPAR * HI
 H_COL = G_COL + N_G
 
@@ -202,7 +234,7 @@
     used = (N_C + 1) // 2 * 2 * HI
     top[used:, :] = jnp.zeros((2 * LANES - used, top.shape[1]), BF16)
     low[used:, :] = jnp.zeros((2 * LANES - used, top.shape[1]), BF16)
-    spread(ci, feats, parts, 0, top, low)
+    spread(ci, feats, parts, (top, 0), (low, 0))
     unit_hot(ci, hot_out)
     hot = hot_out[...]
     both = dot_nt(hot, top[...]) + dot_nt(hot, low[...])
@@ -213,19 +245,25 @@
 
 
 def sweep_kernel(
-    own, left, right, kn, first_in, ph, ap, w, cp, ci, gp, hot, zl, zr, second_out, step_out, z_out, ext, parts, top, low
+    own, inside, outside, kn, first_in, ph, ap, w, cp, ci, gp, hot, zl, zr, second_out, step_out, z_out, ext, parts, mid
 ):
-    lane = lax.broadcasted_iota(jnp.int32, (32, LANES), 1)
-    summed = own[...]
-    summed = summed + jnp.where(lane < 12, pltpu.roll(left[...], 32, 1), 0.0)
-    summed = summed + jnp.where((lane >= 105) & (lane < 117), pltpu.roll(right[...], 96, 1), 0.0)
-    ext[...] = summed
-    row = [ext[r : r + 1, :] for r in range(27)]
+    lane = lax.broadcasted_iota(jnp.int32, own.shape, 1)
     base = jnp.broadcast_to(kn[0:1, 0:1] & ~(KPT - 1), (1, LANES))
+    odd = ((base >> 5) & 1) == 1
+    left = jnp.where(odd, inside[...], outside[...])
+    right = jnp.where(odd, outside[...], inside[...])
+    at_left = lane < HALO + 3
+    at_right = (lane >= HALO + ND) & (lane < HALO + ND + 12)
+    ext[...] = (
+        own[...]
+        + jnp.where(at_left, pltpu.roll(left, LANES - ND, 1), 0.0)
+        + jnp.where(at_right, pltpu.roll(right, ND, 1), 0.0)
+    )
+    row = [ext[r : r + 1, :] for r in range(BAND + 3)]
     node = base + lax.broadcasted_iota(jnp.int32, (1, LANES), 1) - HALO
     exists = (node >= 0) & (node < NODES)
-    rhs = row[0:3]
-    band = [row[3 + 6 * d : 9 + 6 * d] for d in range(4)]
+    rhs = row[BAND:]
+    band = [row[6 * d : 6 * d + 6] for d in range(4)]
     low3, inv3 = factor(band[0], 3)
 
     def precondition(vector):
@@ -268,10 +306,13 @@
     second_out[...] = second
     push = w[...] * second
     feats = [push * cp[a] for a in range(CPAR)]
-    top[...] = jnp.zeros_like(top)
-    low[...] = jnp.zeros_like(low)
-    spread(ci, feats, parts, E_COL, top, low)
-    both = dot_nt(hot[...], top[...]) + dot_nt(hot[...], low[...])
+    half = LANES // 2
+    for row in (E_COL - half // 4, E_COL + half - half // 4):
+        mid[row : row + half // 4, :] = jnp.zeros((half // 4, mid.shape[1]), BF16)
+    spread(ci, feats, parts, (mid, E_COL), (mid, E_COL + half))
+    both = dot_nt(hot[...], mid[...])
+    lane = lax.broadcasted_iota(jnp.int32, both.shape, 1)
+    both = jnp.where((lane >= E_COL) & (lane < G_COL), both + pltpu.roll(both, half, 1), 0.0)
     sums = totals_row([push * gp[a] for a in range(GPAR)], H_COL)
     z_out[pl.ds(0, LO, stride=2), :] = zl[...]
     z_out[pl.ds(1, LO, stride=2), :] = zr[...] + both + sums
@@ -281,14 +322,15 @@
     return pltpu.roll(row, (LANES - start) % LANES, 1) if start else row
 
 
-def solve_kernel(z, row_out, glob_out, fold):
+def solve_kernel(z, row_out, glob_out, step_out, fold):
     parts = [z[8 * k : 8 * k + 8, :] for k in range(z.shape[0] // 8)]
     while len(parts) > 1:
         parts = [a + b for a, b in zip(parts[::2], parts[1::2])]
     fold[...] = parts[0]
     left = fold[0:1, :] + fold[2:3, :] + fold[4:5, :] + fold[6:7, :]
     right = fold[1:2, :] + fold[3:4, :] + fold[5:6, :] + fold[7:8, :]
-    columns = [at_lane(left if f < 16 else right, f * HI % LANES) for f in range(N_C + CPAR)]
+    columns = [at_lane(left if f < 16 else right, f * HI % LANES) for f in range(N_C)]
+    columns += [at_lane(right, E_COL + f * HI) for f in range(CPAR)]
     low6, inv6 = factor(columns[:N_C], CPAR)
     white = forward(low6, inv6, columns[N_C:])
     solved = backward(low6, inv6, white)
@@ -302,8 +344,12 @@
     low4, inv4 = factor(glob[:N_G], GPAR)
     white4 = forward(low4, inv4, glob[N_G:])
     solved4 = backward(low4, inv4, white4)
-    for k, value in enumerate(white4 + solved4):
+    for k, value in enumerate(solved4):
         glob_out[k : k + 1, :] = value
+    row = white4[0]
+    for k in range(1, GPAR):
+        row = jnp.where(lane == k, pltpu.roll(white4[k], k, 1), row)
+    step_out[...] = row[:, :GPAR]
 
 
 def final_kernel(table, second, cp, ci, gp, glob, res_out, calib_out, rows):
@@ -327,78 +373,93 @@
     for c in range(1, CPAR):
         total = total + cp[c] * picked[c]
     out = second[...] - total
-    shift = gp[0] * glob[GPAR : GPAR + 1, 0:1]
+    shift = gp[0] * glob[0:1, 0:1]
     for a in range(1, GPAR):
-        shift = shift + gp[a] * glob[GPAR + a : GPAR + a + 1, 0:1]
+        shift = shift + gp[a] * glob[a : a + 1, 0:1]
     res_out[...] = out - shift
 
 
 NODES = 3072
 
 
-def shifted(x, by):
+def paired(x, start):
     count = lax.axis_size("tm")
-    return lax.ppermute(x, "tm", [(i, i + by) for i in range(count) if 0 <= i + by < count])
-
-
-def call(kernel, outs, scratch, *args, flops=0):
+    low = range(start, count - 1, 2)
+    return lax.ppermute(x, "tm", [(i, i + 1) for i in low] + [(i + 1, i) for i in low])
+
+
+def call(kernel, outs, scratch, *args, flops=0, limit=16 << 20, far=False):
     out_shape = [jax.ShapeDtypeStruct(s, d) for s, d in outs]
+    vmem = pl.BlockSpec(memory_space=pltpu.VMEM)
+    given = pl.BlockSpec(memory_space=pltpu.HBM) if far else vmem
     return pl.pallas_call(
         kernel,
         out_shape=out_shape,
-        scratch_shapes=[pltpu.VMEM(s, d) for s, d in scratch],
+        in_specs=[given] * len(args),
+        out_specs=[vmem] * len(outs),
+        scratch_shapes=scratch,
+        compiler_params=pltpu.CompilerParams(vmem_limit_bytes=limit),
         cost_estimate=pl.CostEstimate(flops=flops, transcendentals=0, bytes_accessed=1 << 20),
-    )(*args)
+    )(*(pltpu.with_memory_space_constraint(a, pltpu.HBM) if far else a for a in args))
 
 
 def per_device(res, w, sp, si, sd, ap, ph, kn, cp, ci, gp):
     tiles = (TILES, LANES)
     rows = TILES * LANES
+    vmem = pltpu.VMEM
     res, w, si, ph, kn, ci = (x.reshape(tiles) for x in (res, w, si, ph, kn, ci))
     sp, ap, cp, gp = (x.reshape(x.shape[0], *tiles) for x in (sp, ap, cp, gp))
     sd = sd.reshape(SPAR, -1, LANES)
-    feat_rows = sum(BASES)
-    padded = -(-feat_rows // 16) * 16
-    first, att = call(
+    groups = lax.axis_size("grp")
+    kept = [(x.shape, x.dtype) for x in (w, ap, ph, kn, cp, ci, gp)]
+    first, copies, w, ap, ph, kn, cp, ci, gp = call(
         attitude_kernel,
-        [(tiles, F32), ((32, LANES), F32)],
-        [((feat_rows * TILES, LANES), F32), ((2 * padded, rows), BF16), ((LANES, rows), BF16), ((padded, LANES), F32)],
-        res, w, sp, si, sd, ap, ph, kn, flops=1 << 24,
-    )
-    groups = lax.axis_size("grp")
-    copies = jnp.broadcast_to(att, (groups, *att.shape))
+        [(tiles, F32), ((groups, 32, LANES), F32)] + kept,
+        [vmem(x.shape, x.dtype) for x in (res, sp, si, sd)]
+        + [
+            vmem((60 * TILES, LANES), F32),
+            vmem((LANES, rows), BF16),
+            vmem((12 * TILES, LANES), F32),
+            vmem((32, rows), BF16),
+            vmem((LANES, rows), BF16),
+            vmem((LANES // 2, LANES), F32),
+            vmem((32, LANES), F32),
+            pltpu.SemaphoreType.DMA((11,)),
+        ],
+        w, ap, ph, kn, cp, ci, gp, res, sp, si, sd, flops=1 << 24, far=True,
+    )
     gathered = lax.all_to_all(copies, "grp", split_axis=0, concat_axis=0, tiled=True)
     zl, zr, hot = call(
         matrix_kernel,
         [((LO, LANES), F32), ((LO, LANES), F32), ((LO, rows), BF16)],
-        [((2, N_C * TILES, LANES), F32), ((2 * LANES, rows), BF16), ((2 * LANES, rows), BF16)],
-        w, cp, ci, gp, flops=1 << 25,
+        [vmem((2, N_C * TILES, LANES), F32), vmem((2 * LANES, rows), BF16), vmem((2 * LANES, rows), BF16)],
+        w, cp, ci, gp, flops=1 << 27,
     )
     own = gathered.sum(axis=0)
-    left = shifted(own, 1)
-    right = shifted(own, -1)
+    outside = paired(own, 1)
+    inside = paired(own, 0)
     second, step, z = call(
         sweep_kernel,
         [(tiles, F32), ((3, ND), F32), ((2 * LO, LANES), F32)],
-        [((32, LANES), F32), ((2, CPAR * TILES, LANES), F32), ((LANES, rows), BF16), ((LANES, rows), BF16)],
-        own, left, right, kn, first, ph, ap, w, cp, ci, gp, hot, zl, zr, flops=1 << 24,
+        [vmem((32, LANES), F32), vmem((2, CPAR * TILES, LANES), F32), vmem((LANES, rows), BF16)],
+        own, inside, outside, kn, first, ph, ap, w, cp, ci, gp, hot, zl, zr, flops=1 << 24,
     )
     both = ("tm", "grp")
     z = lax.all_to_all(z.reshape(LO, 2, LANES), both, split_axis=0, concat_axis=0, tiled=True)
-    copies, glob = call(
+    copies, glob, glob_step = call(
         solve_kernel,
-        [((LO, LANES), F32), ((2 * GPAR, LANES), F32)],
-        [((8, LANES), F32)],
+        [((LO, LANES), F32), ((2 * GPAR, LANES), F32), ((1, GPAR), F32)],
+        [vmem((8, LANES), F32)],
         z.reshape(2 * LO, LANES),
     )
     table = lax.all_to_all(copies.reshape(LO, 1, LANES), both, split_axis=0, concat_axis=0, tiled=True)
     out, calib = call(
         final_kernel,
         [(tiles, F32), ((CPAR, UNITS), F32)],
-        [((LANES, LO), F32)],
+        [vmem((LANES, LO), F32)],
         table.reshape(LO, LANES), second, cp, ci, gp, glob,
     )
-    return out.reshape(1, 1, rows), step, calib, glob[:GPAR, 0]
+    return out.reshape(1, 1, rows), step, calib, glob_step.reshape(GPAR)
 
 
 def solution(mesh):

time: 84.1 us -> 74.5 us (0.89)
  blocking collectives: 41.7 us -> 61.2 us
  waiting for transfers between devices: 11.7 us -> 0.08 us
  Pallas kernels: 14.9 us -> 8 us
  starting transfers between devices: 11.2 us -> 4.3 us
  local copies, waits for them, and re-layouts: 3.27 us -> 0 us
    all_to_all x0 -> x1, blocking collectives: none -> 17.9 us  [per_device(): lax.all_to_all(copies.reshape(LO, 1, LANES), both, split_axis=0, concat_a...]
    all_to_all x1 -> x0, waiting for transfers between devices: 11.7 us -> none  [per_device(): lax.all_to_all(copies.reshape(LO, 1, LANES), both, split_axis=0, concat_a...]
    pallas_call x5, Pallas kernels: 14.9 us -> 8 us  [call(): pl.pallas_call(kernel, out_shape=out_shape, in_specs=[given] * len(args),...]
    all_to_all x1 -> x0, starting transfers between devices: 5.1 us -> none  [per_device(): lax.all_to_all(copies.reshape(LO, 1, LANES), both, split_axis=0, concat_a...]
    ppermute x2, starting transfers between devices: 6.13 us -> 4.3 us  [paired(): lax.ppermute(x, 'tm', [(i, i + 1) for i in low] + [(i + 1, i) for i in low])]
    all_to_all x1, blocking collectives: 27.4 us -> 29 us  [per_device(): lax.all_to_all(z.reshape(LO, 2, LANES), both, split_axis=0, concat_axis=0...]
    slice x1 -> x0, local copies, waits for them, and re-layouts: 1.31 us -> none  [per_device(): return (out.reshape(1, 1, rows), step, calib, glob[:GPAR, 0])]
    unnamed x8 -> x0, local copies, waits for them, and re-layouts: 1.24 us -> none
  transfers between devices with their start and end apart: 3 -> 2, of which waited for: 1 -> 1; matrix products, arithmetic and copies ran while one was open for 2% -> 0% of each run, Pallas kernels for 4% -> 2%
where the time goes in v2:
time: 74.5 us; the launch traced here: 74.3 us
  blocking collectives  61.2 us (82%)
  Pallas kernels  8 us (11%)
  starting transfers between devices  4.3 us (6%)
    all_to_all x1, blocking collectives, per_device(): lax.all_to_all(z.reshape(LO, 2, LANES), both, split_axis=0, concat_axis=0...  29 us
    all_to_all x1, blocking collectives, per_device(): lax.all_to_all(copies.reshape(LO, 1, LANES), both, split_axis=0, concat_a...  17.9 us
    all_to_all x1, blocking collectives, per_device(): lax.all_to_all(copies, 'grp', split_axis=0, concat_axis=0, tiled=True)  14.3 us
    pallas_call x5, Pallas kernels, call(): pl.pallas_call(kernel, out_shape=out_shape, in_specs=[given] * len(args),...  8 us
    ppermute x2, starting transfers between devices, paired(): lax.ppermute(x, 'tm', [(i, i + 1) for i in low] + [(i + 1, i) for i in low])  4.3 us
  transfers between devices with their start and end apart: 2, of which 1 were waited for; matrix products, arithmetic and copies ran while one was open for 0% of the time, Pallas kernels for 2%

profile of v2, /device:TPU:1, one launch (start us, length us, event | category | flops | bytes accessed | tf_op | source)
XLA Modules:
  0.0 74.3 jit_solution(1793273386043656441)
XLA Ops:
  0.6 2.6 %shard_map.138 = (f32[24,128]{1,0:T(8,128)S(1)}, f32[8,32,128]{2,1,0:T(8,128)S(1)}, f32[24,128]{1,0:T(8,128)S(1)}, f32[3,24,128]{2,1,0:T(8,128)S(1)}, f32[24,128...) custom-call(f32[24,128]{1,0:T(8,128)} %bitcast.28, ...), custom_call_target="tpu_custom_call" | custom-call | flops 16777216 | bytes 1048576 | tf_op jit(solution)/shard_map/pallas_call | solution.py:395
  3.2 14.3 %all_to_all.15 = f32[8,32,128]{2,1,0:T(8,128)S(1)} all-to-all(f32[8,32,128]{2,1,0:T(8,128)S(1)} %get-tuple-element.24), channel_id=1, replica_groups=mesh['tm'=32,'grp'=8] {'grp'}, dimensions={0} | all-to-all | bytes 262144 | tf_op jit(solution)/shard_map/all_to_all | solution.py:431
  17.5 4.2 %collective-permute-start.1 = (f32[32,128]{1,0:T(8,128)S(1)}, f32[32,128]{1,0:T(8,128)S(1)}, u32[]{:S(2)}, u32[]{:S(2)}) collective-permute-start(f32[32,128]{1,0:T(8,128)S(1)} %reduce_sum.9.own), channel_id=1, source_target_pairs={{8,16},{24,32},{40,48},{56,64},{72,80},{88,96},{104,112},{120,128}... | collective-permute-start | bytes 49160 | tf_op jit(solution)/shard_map/ppermute | solution.py:388
  21.8 0.1 collective-permute-start
  21.9 1.2 %shard_map.139 = (f32[256,128]{1,0:T(8,128)S(1)}, f32[256,128]{1,0:T(8,128)S(1)}, bf16[256,3072]{1,0:T(8,128)(2,1)S(1)}) custom-call(f32[24,128]{1,0:T(8,128)S(1)} %get-tuple-element.29.w, f32[6,24,128]{2,1,0:T(8,128)S(1)} %get-tuple-element.30.cp, s32[24,128]{1,0:T(8,128)S(1)} %get-tuple-element.31.ci, f32[4,24,128]{2,1,0:T(8,128)S(1)} %get-tuple-element.32.gp), custom_call_target="tpu_custom_call" | custom-call | flops 134217728 | bytes 1048576 | tf_op jit(solution)/shard_map/pallas_call | solution.py:395
  23.1 0.1 collective-permute-done.1.outside
  23.2 0.0 collective-permute-done.inside
  23.2 1.9 %shard_map.140 = (f32[24,128]{1,0:T(8,128)S(1)}, f32[3,96]{1,0:T(4,128)}, f32[512,128]{1,0:T(8,128)S(1)}) custom-call(f32[32,128]{1,0:T(8,128)S(1)} %reduce_sum.9.own, f32[32,128]{1,0:T(8,128)S(1)} %collective-permute-done.inside, f32[32,128]{1,0:T(8,128)S(1)} %collective-permute-done.1.outside, s32[24,128]{1,0:T(8,128)S(1)} %get-tuple-element.25.kn, ...), custom_call_target="tpu_custom_call" | custom-call | flops 16777216 | bytes 1048576 | tf_op jit(solution)/shard_map/pallas_call | solution.py:395
  25.1 29.0 %all_to_all.16 = f32[256,2,128]{2,1,0:T(2,128)S(1)} all-to-all(f32[256,2,128]{2,1,0:T(2,128)S(1)} %bitcast.21), channel_id=1, replica_groups=mesh['tm'=32,'grp'=8] {'tm','grp'}, dimensions={0} | all-to-all | bytes 524288 | tf_op jit(solution)/shard_map/all_to_all | solution.py:448
  54.1 0.8 %shard_map.141 = (f32[256,128]{1,0:T(8,128)S(1)}, f32[8,128]{1,0:T(8,128)S(1)}, f32[1,4]{1,0:T(1,128)}) custom-call(f32[512,128]{1,0:T(8,128)S(1)} %bitcast.19), custom_call_target="tpu_custom_call" | custom-call | bytes 1048576 | tf_op jit(solution)/shard_map/pallas_call | solution.py:395
  54.9 17.9 %all_to_all.17 = f32[256,1,128]{2,1,0:T(1,128)S(1)} all-to-all(f32[256,1,128]{2,1,0:T(1,128)S(1)} %bitcast.22), channel_id=1, replica_groups=mesh['tm'=32,'grp'=8] {'tm','grp'}, dimensions={0} | all-to-all | bytes 262144 | tf_op jit(solution)/shard_map/all_to_all | solution.py:455
  72.8 1.5 %shard_map.142 = (f32[24,128]{1,0:T(8,128)}, f32[6,2048]{1,0:T(8,128)}) custom-call(f32[256,128]{1,0:T(8,128)S(1)} %bitcast.20, f32[24,128]{1,0:T(8,128)S(1)} %get-tuple-element.38.second, f32[6,24,128]{2,1,0:T(8,128)S(1)} %get-tuple-element.30.cp, s32[24,128]{1,0:T(8,128)S(1)} %get-tuple-element.31.ci, f32[4,24,128]{2,1,0:T(8,128)S(1)} %get-tuple-element.32.gp, ...), custom_call_target="tpu_custom_call" | custom-call | bytes 1048576 | tf_op jit(solution)/shard_map/pallas_call | solution.py:395
  (1 shorter events, 0.0 us)
Async XLA Ops:
  17.5 5.6 %collective-permute-start.1 = (f32[32,128]{1,0:T(8,128)S(1)}, f32[32,128]{1,0:T(8,128)S(1)}, u32[]{:S(2)}, u32[]{:S(2)}) collective-permute-start(f32[32,128]{1,0:T(8,128)S(1)} %reduce_sum.9.own), channel_id=1, source_target_pairs={{8,16},{24,32},{40,48},{56,64},{72,80},{88,96},{104,112},{120,128}... | collective-permute-start | bytes 49160 | tf_op jit(solution)/shard_map/ppermute | solution.py:388
  21.8 1.4 %collective-permute-start = (f32[32,128]{1,0:T(8,128)S(1)}, f32[32,128]{1,0:T(8,128)S(1)}, u32[]{:S(2)}, u32[]{:S(2)}) collective-permute-start(f32[32,128]{1,0:T(8,128)S(1)} %reduce_sum.9.own), channel_id=1, source_target_pairs={{0,8},{16,24},{32,40},{48,56},{64,72},{80,88},{96,104},{112,120},{... | collective-permute-start | bytes 49160 | tf_op jit(solution)/shard_map/ppermute | solution.py:388

commit v3 on v2

--- a/solution.py
+++ b/solution.py
@@ -3,6 +3,7 @@
 from jax import lax
 from jax.experimental import pallas as pl
 from jax.experimental.pallas import tpu as pltpu
+from jax.sharding import Mesh
 from jax.sharding import PartitionSpec as P
 
 LANES = 128
@@ -178,11 +179,11 @@
         loads[i].wait()
 
 
-def unit_hot(unit, hot):
+def unit_hot(unit, flip, hot):
     lo_id = lax.broadcasted_iota(jnp.int32, (LO, LANES), 0)
     for t in range(TILES):
         cols = slice(t * LANES, (t + 1) * LANES)
-        lo = unit[t : t + 1, :] & (LO - 1)
+        lo = (unit[t : t + 1, :] & (LO - 1)) ^ flip
         hot[:, cols] = jnp.where(lo_id == lo, 1.0, 0.0).astype(BF16)
 
 
@@ -226,7 +227,7 @@
 H_COL = G_COL + N_G
 
 
-def matrix_kernel(w, cp, ci, gp, left_out, right_out, hot_out, parts, top, low):
+def matrix_kernel(w, cp, ci, gp, kn, left_out, right_out, hot_out, parts, top, low):
     weight = w[...]
     calib = [cp[a] for a in range(CPAR)]
     weighted = [weight * c for c in calib]
@@ -235,7 +236,8 @@
     top[used:, :] = jnp.zeros((2 * LANES - used, top.shape[1]), BF16)
     low[used:, :] = jnp.zeros((2 * LANES - used, top.shape[1]), BF16)
     spread(ci, feats, parts, (top, 0), (low, 0))
-    unit_hot(ci, hot_out)
+    flip = ((kn[0:1, 0:1] >> 5) & 1) << 7
+    unit_hot(ci, jnp.broadcast_to(flip, (1, LANES)), hot_out)
     hot = hot_out[...]
     both = dot_nt(hot, top[...]) + dot_nt(hot, low[...])
     glob = [gp[a] for a in range(GPAR)]
@@ -245,7 +247,7 @@
 
 
 def sweep_kernel(
-    own, inside, outside, kn, first_in, ph, ap, w, cp, ci, gp, hot, zl, zr, second_out, step_out, z_out, ext, parts, mid
+    own, inside, outside, kn, first_in, ph, ap, w, cp, ci, gp, hot, zl, zr, second_out, step_out, keep_out, send_out, ext, parts, mid
 ):
     lane = lax.broadcasted_iota(jnp.int32, own.shape, 1)
     base = jnp.broadcast_to(kn[0:1, 0:1] & ~(KPT - 1), (1, LANES))
@@ -310,12 +312,15 @@
     for row in (E_COL - half // 4, E_COL + half - half // 4):
         mid[row : row + half // 4, :] = jnp.zeros((half // 4, mid.shape[1]), BF16)
     spread(ci, feats, parts, (mid, E_COL), (mid, E_COL + half))
-    both = dot_nt(hot[...], mid[...])
+    both = dot_nt(mid[...], hot[...])
+    both = jnp.concatenate([jnp.transpose(both[:, :LANES]), jnp.transpose(both[:, LANES:])], axis=0)
     lane = lax.broadcasted_iota(jnp.int32, both.shape, 1)
     both = jnp.where((lane >= E_COL) & (lane < G_COL), both + pltpu.roll(both, half, 1), 0.0)
     sums = totals_row([push * gp[a] for a in range(GPAR)], H_COL)
-    z_out[pl.ds(0, LO, stride=2), :] = zl[...]
-    z_out[pl.ds(1, LO, stride=2), :] = zr[...] + both + sums
+    right = zr[...] + both + sums
+    for to, at in ((keep_out, 0), (send_out, LO // 2)):
+        to[pl.ds(0, LO // 2, stride=2), :] = zl[at : at + LO // 2, :]
+        to[pl.ds(1, LO // 2, stride=2), :] = right[at : at + LO // 2, :]
 
 
 def at_lane(row, start):
@@ -353,8 +358,9 @@
 
 
 def final_kernel(table, second, cp, ci, gp, glob, res_out, calib_out, rows):
-    rows[:, 0:LANES] = jnp.transpose(table[0:LANES, :])
-    rows[:, LANES:] = jnp.transpose(table[LANES:, :])
+    for core in range(2):
+        held = [table[16 * p + 8 * core : 16 * p + 8 * core + 8, :] for p in range(LO // 16)]
+        rows[:, core * LANES : (core + 1) * LANES] = jnp.transpose(jnp.concatenate(held, axis=0))
     for j in range(CPAR):
         for h in range(HI):
             calib_out[j : j + 1, h * LO : (h + 1) * LO] = rows[j * HI + h : j * HI + h + 1, :]
@@ -380,12 +386,13 @@
 
 
 NODES = 3072
+TM = ("pair", "core")
 
 
 def paired(x, start):
-    count = lax.axis_size("tm")
+    count = lax.axis_size(TM)
     low = range(start, count - 1, 2)
-    return lax.ppermute(x, "tm", [(i, i + 1) for i in low] + [(i + 1, i) for i in low])
+    return lax.ppermute(x, TM, [(i, i + 1) for i in low] + [(i + 1, i) for i in low])
 
 
 def call(kernel, outs, scratch, *args, flops=0, limit=16 << 20, far=False):
@@ -433,26 +440,26 @@
         matrix_kernel,
         [((LO, LANES), F32), ((LO, LANES), F32), ((LO, rows), BF16)],
         [vmem((2, N_C * TILES, LANES), F32), vmem((2 * LANES, rows), BF16), vmem((2 * LANES, rows), BF16)],
-        w, cp, ci, gp, flops=1 << 27,
+        w, cp, ci, gp, kn, flops=1 << 27,
     )
     own = gathered.sum(axis=0)
     outside = paired(own, 1)
     inside = paired(own, 0)
-    second, step, z = call(
+    second, step, keep, send = call(
         sweep_kernel,
-        [(tiles, F32), ((3, ND), F32), ((2 * LO, LANES), F32)],
+        [(tiles, F32), ((3, ND), F32), ((LO, LANES), F32), ((LO, LANES), F32)],
         [vmem((32, LANES), F32), vmem((2, CPAR * TILES, LANES), F32), vmem((LANES, rows), BF16)],
         own, inside, outside, kn, first, ph, ap, w, cp, ci, gp, hot, zl, zr, flops=1 << 24,
     )
-    both = ("tm", "grp")
-    z = lax.all_to_all(z.reshape(LO, 2, LANES), both, split_axis=0, concat_axis=0, tiled=True)
+    z = (keep + paired(send, 0)).reshape(LO // 2, 2, LANES)
+    z = lax.all_to_all(z, ("pair", "grp"), split_axis=0, concat_axis=0, tiled=True)
     copies, glob, glob_step = call(
         solve_kernel,
         [((LO, LANES), F32), ((2 * GPAR, LANES), F32), ((1, GPAR), F32)],
         [vmem((8, LANES), F32)],
-        z.reshape(2 * LO, LANES),
-    )
-    table = lax.all_to_all(copies.reshape(LO, 1, LANES), both, split_axis=0, concat_axis=0, tiled=True)
+        z.reshape(LO, LANES),
+    )
+    table = lax.all_to_all(copies.reshape(LO, 1, LANES), (*TM, "grp"), split_axis=0, concat_axis=0, tiled=True)
     out, calib = call(
         final_kernel,
         [(tiles, F32), ((CPAR, UNITS), F32)],
@@ -463,22 +470,24 @@
 
 
 def solution(mesh):
+    count, groups = mesh.devices.shape
+    mesh = Mesh(mesh.devices.reshape(count // 2, 2, groups), (*TM, "grp"))
     return jax.shard_map(
         per_device,
         mesh=mesh,
         in_specs=(
-            P("tm", "grp", None),
-            P("tm", "grp", None),
-            P(None, "tm", "grp", None),
-            P("tm", "grp", None),
-            P(None, "tm", None),
-            P(None, "tm", "grp", None),
-            P("tm", "grp", None),
-            P("tm", "grp", None),
-            P(None, "tm", "grp", None),
-            P("tm", "grp", None),
-            P(None, "tm", "grp", None),
+            P(TM, "grp", None),
+            P(TM, "grp", None),
+            P(None, TM, "grp", None),
+            P(TM, "grp", None),
+            P(None, TM, None),
+            P(None, TM, "grp", None),
+            P(TM, "grp", None),
+            P(TM, "grp", None),
+            P(None, TM, "grp", None),
+            P(TM, "grp", None),
+            P(None, TM, "grp", None),
         ),
-        out_specs=(P("tm", "grp", None), P(None, "tm"), P(), P()),
+        out_specs=(P(TM, "grp", None), P(None, TM), P(), P()),
         check_vma=False,
     )

time: 74.5 us -> 73.5 us (0.987)
  blocking collectives: 61.2 us -> 59.1 us
  waiting for transfers between devices: 0.08 us -> 1.03 us
    all_to_all x2, blocking collectives: 46.9 us -> 44.8 us  [the longest x1 25 us: per_device(): lax.all_to_all(z, ('pair', 'grp'), split_axis=0, concat_axis=0, tiled=True)]
    ppermute x2 -> x3, waiting for transfers between devices: 0.08 us -> 1.03 us  [paired(): lax.ppermute(x, TM, [(i, i + 1) for i in low] + [(i + 1, i) for i in low])]
    ppermute x2 -> x3, starting transfers between devices: 4.3 us -> 4.86 us  [paired(): lax.ppermute(x, TM, [(i, i + 1) for i in low] + [(i + 1, i) for i in low])]
  transfers between devices with their start and end apart: 2 -> 3, of which waited for: 1 -> 1; matrix products, arithmetic and copies ran while one was open for 0% -> 0% of each run, Pallas kernels for 2% -> 2%
where the time goes in v3:
time: 73.5 us; the launch traced here: 73.3 us
  blocking collectives  59.1 us (80%)
  Pallas kernels  7.55 us (10%)
  starting transfers between devices  4.86 us (7%)
  waiting for transfers between devices  1.03 us (1%)
    all_to_all x1, blocking collectives, per_device(): lax.all_to_all(z, ('pair', 'grp'), split_axis=0, concat_axis=0, tiled=True)  25 us
    all_to_all x1, blocking collectives, per_device(): lax.all_to_all(copies.reshape(LO, 1, LANES), (*TM, 'grp'), split_axis=0,...  19.8 us
    all_to_all x1, blocking collectives, per_device(): lax.all_to_all(copies, 'grp', split_axis=0, concat_axis=0, tiled=True)  14.3 us
    pallas_call x5, Pallas kernels, call(): pl.pallas_call(kernel, out_shape=out_shape, in_specs=[given] * len(args),...  7.55 us
    ppermute x3, starting transfers between devices, paired(): lax.ppermute(x, TM, [(i, i + 1) for i in low] + [(i + 1, i) for i in low])  4.86 us
  transfers between devices with their start and end apart: 3, of which 1 were waited for; matrix products, arithmetic and copies ran while one was open for 0% of the time, Pallas kernels for 2%

profile of v3, /device:TPU:1, one launch (start us, length us, event | category | flops | bytes accessed | tf_op | source)
XLA Modules:
  0.0 73.3 jit_solution(947930927782645091)
XLA Ops:
  0.6 2.6 %shard_map.138 = (f32[24,128]{1,0:T(8,128)S(1)}, f32[8,32,128]{2,1,0:T(8,128)S(1)}, f32[24,128]{1,0:T(8,128)S(1)}, f32[3,24,128]{2,1,0:T(8,128)S(1)}, f32[24,128...) custom-call(f32[24,128]{1,0:T(8,128)} %bitcast.28, ...), custom_call_target="tpu_custom_call" | custom-call | flops 16777216 | bytes 1048576 | tf_op jit(solution)/shard_map/pallas_call | solution.py:402
  3.2 14.3 %all_to_all.15 = f32[8,32,128]{2,1,0:T(8,128)S(1)} all-to-all(f32[8,32,128]{2,1,0:T(8,128)S(1)} %get-tuple-element.25), channel_id=1, replica_groups=mesh['pair'=16,'core'=2,'grp'=8] {'grp'}, dimensions={0} | all-to-all | bytes 262144 | tf_op jit(solution)/shard_map/all_to_all | solution.py:438
  17.5 4.2 %collective-permute-start.1 = (f32[32,128]{1,0:T(8,128)S(1)}, f32[32,128]{1,0:T(8,128)S(1)}, u32[]{:S(2)}, u32[]{:S(2)}) collective-permute-start(f32[32,128]{1,0:T(8,128)S(1)} %reduce_sum.9.own), channel_id=1, source_target_pairs={{8,16},{24,32},{40,48},{56,64},{72,80},{88,96},{104,112},{120,128}... | collective-permute-start | bytes 49160 | tf_op jit(solution)/shard_map/ppermute | solution.py:395
  21.8 0.1 collective-permute-start
  21.9 1.3 %shard_map.139 = (f32[256,128]{1,0:T(8,128)S(1)}, f32[256,128]{1,0:T(8,128)S(1)}, bf16[256,3072]{1,0:T(8,128)(2,1)S(1)}) custom-call(f32[24,128]{1,0:T(8,128)S(1)} %get-tuple-element.30.w, f32[6,24,128]{2,1,0:T(8,128)S(1)} %get-tuple-element.31.cp, s32[24,128]{1,0:T(8,128)S(1)} %get-tuple-element.32.ci, f32[4,24,128]{2,1,0:T(8,128)S(1)} %get-tuple-element.33.gp, ...), custom_call_target="tpu_custom_call" | custom-call | flops 134217728 | bytes 1048576 | tf_op jit(solution)/shard_map/pallas_call | solution.py:402
  23.1 0.0 collective-permute-done.1.outside
  23.2 0.0 collective-permute-done.inside
  23.2 1.4 %shard_map.140 = (f32[24,128]{1,0:T(8,128)S(1)}, f32[3,96]{1,0:T(4,128)}, f32[256,128]{1,0:T(8,128)S(1)}, f32[256,128]{1,0:T(8,128)S(1)}) custom-call(f32[32,128]{1,0:T(8,128)S(1)} %reduce_sum.9.own, f32[32,128]{1,0:T(8,128)S(1)} %collective-permute-done.inside, f32[32,128]{1,0:T(8,128)S(1)} %collective-permute-done.1.outside, ...), custom_call_target="tpu_custom_call" | custom-call | flops 16777216 | bytes 1048576 | tf_op jit(solution)/shard_map/pallas_call | solution.py:402
  24.6 0.6 collective-permute-start.2
  25.2 1.0 %collective-permute-done.2 = f32[256,128]{1,0:T(8,128)S(1)} collective-permute-done((f32[256,128]{1,0:T(8,128)S(1)}, f32[256,128]{1,0:T(8,128)S(1)}, u32[]{:S(2)}, u32[]{:S(2)}) %collective-permute-start.2) | collective-permute-done | bytes 131104 | tf_op jit(solution)/shard_map/ppermute | solution.py:395
  26.2 25.0 %all_to_all.16 = f32[128,2,128]{2,1,0:T(2,128)S(1)} all-to-all(f32[128,2,128]{2,1,0:T(2,128)S(1)} %bitcast.22), channel_id=1, replica_groups=mesh['pair'=16,'core'=2,'grp'=8] {'pair','grp'}, dimensions={0} | all-to-all | bytes 262144 | tf_op jit(solution)/shard_map/all_to_all | solution.py:455
  51.1 0.8 %shard_map.141 = (f32[256,128]{1,0:T(8,128)S(1)}, f32[8,128]{1,0:T(8,128)S(1)}, f32[1,4]{1,0:T(1,128)}) custom-call(f32[256,128]{1,0:T(8,128)S(1)} %bitcast.20), custom_call_target="tpu_custom_call" | custom-call | bytes 1048576 | tf_op jit(solution)/shard_map/pallas_call | solution.py:402
  51.9 19.8 %all_to_all.17 = f32[256,1,128]{2,1,0:T(1,128)S(1)} all-to-all(f32[256,1,128]{2,1,0:T(1,128)S(1)} %bitcast.21), channel_id=1, replica_groups=mesh['pair'=16,'core'=2,'grp'=8] {'pair','core','grp'}, dimensions={0} | all-to-all | bytes 262144 | tf_op jit(solution)/shard_map/all_to_all | solution.py:462
  71.7 1.5 %shard_map.142 = (f32[24,128]{1,0:T(8,128)}, f32[6,2048]{1,0:T(8,128)}) custom-call(f32[256,128]{1,0:T(8,128)S(1)} %bitcast.19, f32[24,128]{1,0:T(8,128)S(1)} %get-tuple-element.40.second, f32[6,24,128]{2,1,0:T(8,128)S(1)} %get-tuple-element.31.cp, s32[24,128]{1,0:T(8,128)S(1)} %get-tuple-element.32.ci, f32[4,24,128]{2,1,0:T(8,128)S(1)} %get-tuple-element.33.gp, ...), custom_call_target="tpu_custom_call" | custom-call | bytes 1048576 | tf_op jit(solution)/shard_map/pallas_call | solution.py:402
  (2 shorter events, 0.0 us)
Async XLA Ops:
  17.5 5.6 %collective-permute-start.1 = (f32[32,128]{1,0:T(8,128)S(1)}, f32[32,128]{1,0:T(8,128)S(1)}, u32[]{:S(2)}, u32[]{:S(2)}) collective-permute-start(f32[32,128]{1,0:T(8,128)S(1)} %reduce_sum.9.own), channel_id=1, source_target_pairs={{8,16},{24,32},{40,48},{56,64},{72,80},{88,96},{104,112},{120,128}... | collective-permute-start | bytes 49160 | tf_op jit(solution)/shard_map/ppermute | solution.py:395
  21.8 1.4 %collective-permute-start = (f32[32,128]{1,0:T(8,128)S(1)}, f32[32,128]{1,0:T(8,128)S(1)}, u32[]{:S(2)}, u32[]{:S(2)}) collective-permute-start(f32[32,128]{1,0:T(8,128)S(1)} %reduce_sum.9.own), channel_id=1, source_target_pairs={{0,8},{16,24},{32,40},{48,56},{64,72},{80,88},{96,104},{112,120},{... | collective-permute-start | bytes 49160 | tf_op jit(solution)/shard_map/ppermute | solution.py:395
  24.6 1.5 %collective-permute-start.2 = (f32[256,128]{1,0:T(8,128)S(1)}, f32[256,128]{1,0:T(8,128)S(1)}, u32[]{:S(2)}, u32[]{:S(2)}) collective-permute-start(f32[256,128]{1,0:T(8,128)S(1)} %get-tuple-element.38), channel_id=1, source_target_pairs={{0,8},{16,24},{32,40},{48,56},{64,72},{80,88},{96,104},{112,120},{... | collective-permute-start | bytes 393224 | tf_op jit(solution)/shard_map/ppermute | solution.py:395

commit v4 on v3

--- a/solution.py
+++ b/solution.py
@@ -91,6 +91,11 @@
 def halves(x):
     top = x.astype(BF16).astype(F32)
     return top, x - top
+
+
+def thirds(x):
+    top, rest = halves(x)
+    return (top, *halves(rest))
 
 
 def dot_nt(a, b):
@@ -157,11 +162,10 @@
             at += 1
     for t in range(TILES):
         cols = slice(t * LANES, (t + 1) * LANES)
-        top, low = halves(rhs_feat[pl.ds(t, at, stride=TILES), :])
-        rhs[0:at, cols] = top.astype(BF16)
-        rhs[16 : 16 + at, cols] = low.astype(BF16)
+        for k, part in enumerate(thirds(rhs_feat[pl.ds(t, at, stride=TILES), :])):
+            rhs[16 * k : 16 * k + at, cols] = part.astype(BF16)
     both = dot_nt(rhs[...], hot[...])
-    both = both[:16] + both[16:]
+    both = both[:16] + (both[16:32] + both[32:])
     shut[...] = jnp.zeros_like(shut)
     at = 0
     side = both[0:3]
@@ -187,17 +191,16 @@
         hot[:, cols] = jnp.where(lo_id == lo, 1.0, 0.0).astype(BF16)
 
 
-def spread(unit, feats, parts, top_to, low_to):
+def spread(unit, feats, parts, split, *places):
     for f, value in enumerate(feats):
-        top, low = halves(value)
-        parts[0, pl.ds(f * TILES, TILES), :] = top
-        parts[1, pl.ds(f * TILES, TILES), :] = low
+        for k, part in enumerate(split(value)):
+            parts[k, pl.ds(f * TILES, TILES), :] = part
     hi_id = lax.broadcasted_iota(jnp.int32, (HI, LANES), 0)
     zero = jnp.zeros((HI, LANES), F32)
     for t in range(TILES):
         cols = slice(t * LANES, (t + 1) * LANES)
         mine = hi_id == (unit[t : t + 1, :] >> 8)
-        for part, (to, base) in ((0, top_to), (1, low_to)):
+        for part, (to, base) in enumerate(places):
             for f in range(0, len(feats), 2):
                 rows = []
                 for g in (f, f + 1):
@@ -206,7 +209,7 @@
                         rows.append(jnp.where(mine, jnp.broadcast_to(row, (HI, LANES)), 0.0))
                     else:
                         rows.append(zero)
-                at = (base + f * HI) % to.shape[0]
+                at = base + f * HI
                 to[at : at + 2 * HI, cols] = jnp.concatenate(rows, axis=0).astype(BF16)
 
 
@@ -235,7 +238,7 @@
     used = (N_C + 1) // 2 * 2 * HI
     top[used:, :] = jnp.zeros((2 * LANES - used, top.shape[1]), BF16)
     low[used:, :] = jnp.zeros((2 * LANES - used, top.shape[1]), BF16)
-    spread(ci, feats, parts, (top, 0), (low, 0))
+    spread(ci, feats, parts, halves, (top, 0), (low, 0))
     flip = ((kn[0:1, 0:1] >> 5) & 1) << 7
     unit_hot(ci, jnp.broadcast_to(flip, (1, LANES)), hot_out)
     hot = hot_out[...]
@@ -308,14 +311,14 @@
     second_out[...] = second
     push = w[...] * second
     feats = [push * cp[a] for a in range(CPAR)]
-    half = LANES // 2
-    for row in (E_COL - half // 4, E_COL + half - half // 4):
-        mid[row : row + half // 4, :] = jnp.zeros((half // 4, mid.shape[1]), BF16)
-    spread(ci, feats, parts, (mid, E_COL), (mid, E_COL + half))
+    span = CPAR * HI
+    spread(ci, feats, parts, thirds, *((mid, k * span) for k in range(3)))
     both = dot_nt(mid[...], hot[...])
+    both = both[:span] + (both[span : 2 * span] + both[2 * span :])
+    above = jnp.zeros((E_COL, LO), F32)
+    below = jnp.zeros((LANES - G_COL, LO), F32)
+    both = jnp.concatenate([above, both, below], axis=0)
     both = jnp.concatenate([jnp.transpose(both[:, :LANES]), jnp.transpose(both[:, LANES:])], axis=0)
-    lane = lax.broadcasted_iota(jnp.int32, both.shape, 1)
-    both = jnp.where((lane >= E_COL) & (lane < G_COL), both + pltpu.roll(both, half, 1), 0.0)
     sums = totals_row([push * gp[a] for a in range(GPAR)], H_COL)
     right = zr[...] + both + sums
     for to, at in ((keep_out, 0), (send_out, LO // 2)):
@@ -427,7 +430,7 @@
             vmem((60 * TILES, LANES), F32),
             vmem((LANES, rows), BF16),
             vmem((12 * TILES, LANES), F32),
-            vmem((32, rows), BF16),
+            vmem((48, rows), BF16),
             vmem((LANES, rows), BF16),
             vmem((LANES // 2, LANES), F32),
             vmem((32, LANES), F32),
@@ -448,7 +451,7 @@
     second, step, keep, send = call(
         sweep_kernel,
         [(tiles, F32), ((3, ND), F32), ((LO, LANES), F32), ((LO, LANES), F32)],
-        [vmem((32, LANES), F32), vmem((2, CPAR * TILES, LANES), F32), vmem((LANES, rows), BF16)],
+        [vmem((32, LANES), F32), vmem((3, CPAR * TILES, LANES), F32), vmem((3 * CPAR * HI, rows), BF16)],
         own, inside, outside, kn, first, ph, ap, w, cp, ci, gp, hot, zl, zr, flops=1 << 24,
     )
     z = (keep + paired(send, 0)).reshape(LO // 2, 2, LANES)

time: 73.5 us -> 73.5 us (level)
  no operation moved by 1% of the time
where the time goes in v4:
time: 73.5 us; the launch traced here: 73.2 us
  blocking collectives  59.1 us (80%)
  Pallas kernels  7.51 us (10%)
  starting transfers between devices  4.86 us (7%)
  waiting for transfers between devices  1.03 us (1%)
    all_to_all x1, blocking collectives, per_device(): lax.all_to_all(z, ('pair', 'grp'), split_axis=0, concat_axis=0, tiled=True)  25 us
    all_to_all x1, blocking collectives, per_device(): lax.all_to_all(copies.reshape(LO, 1, LANES), (*TM, 'grp'), split_axis=0,...  19.8 us
    all_to_all x1, blocking collectives, per_device(): lax.all_to_all(copies, 'grp', split_axis=0, concat_axis=0, tiled=True)  14.3 us
    pallas_call x5, Pallas kernels, call(): pl.pallas_call(kernel, out_shape=out_shape, in_specs=[given] * len(args),...  7.51 us
    ppermute x3, starting transfers between devices, paired(): lax.ppermute(x, TM, [(i, i + 1) for i in low] + [(i + 1, i) for i in low])  4.86 us
  transfers between devices with their start and end apart: 3, of which 1 were waited for; matrix products, arithmetic and copies ran while one was open for 0% of the time, Pallas kernels for 2%

profile of v4, /device:TPU:1, one launch (start us, length us, event | category | flops | bytes accessed | tf_op | source)
XLA Modules:
  0.0 73.2 jit_solution(5530886049276638401)
XLA Ops:
  0.6 2.6 %shard_map.138 = (f32[24,128]{1,0:T(8,128)S(1)}, f32[8,32,128]{2,1,0:T(8,128)S(1)}, f32[24,128]{1,0:T(8,128)S(1)}, f32[3,24,128]{2,1,0:T(8,128)S(1)}, f32[24,128...) custom-call(f32[24,128]{1,0:T(8,128)} %bitcast.28, ...), custom_call_target="tpu_custom_call" | custom-call | flops 16777216 | bytes 1048576 | tf_op jit(solution)/shard_map/pallas_call | solution.py:405
  3.2 14.3 %all_to_all.15 = f32[8,32,128]{2,1,0:T(8,128)S(1)} all-to-all(f32[8,32,128]{2,1,0:T(8,128)S(1)} %get-tuple-element.25), channel_id=1, replica_groups=mesh['pair'=16,'core'=2,'grp'=8] {'grp'}, dimensions={0} | all-to-all | bytes 262144 | tf_op jit(solution)/shard_map/all_to_all | solution.py:441
  17.6 4.2 %collective-permute-start.1 = (f32[32,128]{1,0:T(8,128)S(1)}, f32[32,128]{1,0:T(8,128)S(1)}, u32[]{:S(2)}, u32[]{:S(2)}) collective-permute-start(f32[32,128]{1,0:T(8,128)S(1)} %reduce_sum.9.own), channel_id=1, source_target_pairs={{8,16},{24,32},{40,48},{56,64},{72,80},{88,96},{104,112},{120,128}... | collective-permute-start | bytes 49160 | tf_op jit(solution)/shard_map/ppermute | solution.py:398
  21.8 0.1 collective-permute-start
  21.9 1.3 %shard_map.139 = (f32[256,128]{1,0:T(8,128)S(1)}, f32[256,128]{1,0:T(8,128)S(1)}, bf16[256,3072]{1,0:T(8,128)(2,1)S(1)}) custom-call(f32[24,128]{1,0:T(8,128)S(1)} %get-tuple-element.30.w, f32[6,24,128]{2,1,0:T(8,128)S(1)} %get-tuple-element.31.cp, s32[24,128]{1,0:T(8,128)S(1)} %get-tuple-element.32.ci, f32[4,24,128]{2,1,0:T(8,128)S(1)} %get-tuple-element.33.gp, ...), custom_call_target="tpu_custom_call" | custom-call | flops 134217728 | bytes 1048576 | tf_op jit(solution)/shard_map/pallas_call | solution.py:405
  23.1 0.0 collective-permute-done.1.outside
  23.2 0.0 collective-permute-done.inside
  23.2 1.4 %shard_map.140 = (f32[24,128]{1,0:T(8,128)S(1)}, f32[3,96]{1,0:T(4,128)}, f32[256,128]{1,0:T(8,128)S(1)}, f32[256,128]{1,0:T(8,128)S(1)}) custom-call(f32[32,128]{1,0:T(8,128)S(1)} %reduce_sum.9.own, f32[32,128]{1,0:T(8,128)S(1)} %collective-permute-done.inside, f32[32,128]{1,0:T(8,128)S(1)} %collective-permute-done.1.outside, ...), custom_call_target="tpu_custom_call" | custom-call | flops 16777216 | bytes 1048576 | tf_op jit(solution)/shard_map/pallas_call | solution.py:405
  24.6 0.6 collective-permute-start.2
  25.1 1.0 %collective-permute-done.2 = f32[256,128]{1,0:T(8,128)S(1)} collective-permute-done((f32[256,128]{1,0:T(8,128)S(1)}, f32[256,128]{1,0:T(8,128)S(1)}, u32[]{:S(2)}, u32[]{:S(2)}) %collective-permute-start.2) | collective-permute-done | bytes 131104 | tf_op jit(solution)/shard_map/ppermute | solution.py:398
  26.1 25.0 %all_to_all.16 = f32[128,2,128]{2,1,0:T(2,128)S(1)} all-to-all(f32[128,2,128]{2,1,0:T(2,128)S(1)} %bitcast.22), channel_id=1, replica_groups=mesh['pair'=16,'core'=2,'grp'=8] {'pair','grp'}, dimensions={0} | all-to-all | bytes 262144 | tf_op jit(solution)/shard_map/all_to_all | solution.py:458
  51.1 0.8 %shard_map.141 = (f32[256,128]{1,0:T(8,128)S(1)}, f32[8,128]{1,0:T(8,128)S(1)}, f32[1,4]{1,0:T(1,128)}) custom-call(f32[256,128]{1,0:T(8,128)S(1)} %bitcast.20), custom_call_target="tpu_custom_call" | custom-call | bytes 1048576 | tf_op jit(solution)/shard_map/pallas_call | solution.py:405
  51.9 19.8 %all_to_all.17 = f32[256,1,128]{2,1,0:T(1,128)S(1)} all-to-all(f32[256,1,128]{2,1,0:T(1,128)S(1)} %bitcast.21), channel_id=1, replica_groups=mesh['pair'=16,'core'=2,'grp'=8] {'pair','core','grp'}, dimensions={0} | all-to-all | bytes 262144 | tf_op jit(solution)/shard_map/all_to_all | solution.py:465
  71.7 1.5 %shard_map.142 = (f32[24,128]{1,0:T(8,128)}, f32[6,2048]{1,0:T(8,128)}) custom-call(f32[256,128]{1,0:T(8,128)S(1)} %bitcast.19, f32[24,128]{1,0:T(8,128)S(1)} %get-tuple-element.40.second, f32[6,24,128]{2,1,0:T(8,128)S(1)} %get-tuple-element.31.cp, s32[24,128]{1,0:T(8,128)S(1)} %get-tuple-element.32.ci, f32[4,24,128]{2,1,0:T(8,128)S(1)} %get-tuple-element.33.gp, ...), custom_call_target="tpu_custom_call" | custom-call | bytes 1048576 | tf_op jit(solution)/shard_map/pallas_call | solution.py:405
  (2 shorter events, 0.0 us)
Async XLA Ops:
  17.6 5.6 %collective-permute-start.1 = (f32[32,128]{1,0:T(8,128)S(1)}, f32[32,128]{1,0:T(8,128)S(1)}, u32[]{:S(2)}, u32[]{:S(2)}) collective-permute-start(f32[32,128]{1,0:T(8,128)S(1)} %reduce_sum.9.own), channel_id=1, source_target_pairs={{8,16},{24,32},{40,48},{56,64},{72,80},{88,96},{104,112},{120,128}... | collective-permute-start | bytes 49160 | tf_op jit(solution)/shard_map/ppermute | solution.py:398
  21.8 1.4 %collective-permute-start = (f32[32,128]{1,0:T(8,128)S(1)}, f32[32,128]{1,0:T(8,128)S(1)}, u32[]{:S(2)}, u32[]{:S(2)}) collective-permute-start(f32[32,128]{1,0:T(8,128)S(1)} %reduce_sum.9.own), channel_id=1, source_target_pairs={{0,8},{16,24},{32,40},{48,56},{64,72},{80,88},{96,104},{112,120},{... | collective-permute-start | bytes 49160 | tf_op jit(solution)/shard_map/ppermute | solution.py:398
  24.6 1.5 %collective-permute-start.2 = (f32[256,128]{1,0:T(8,128)S(1)}, f32[256,128]{1,0:T(8,128)S(1)}, u32[]{:S(2)}, u32[]{:S(2)}) collective-permute-start(f32[256,128]{1,0:T(8,128)S(1)} %get-tuple-element.38), channel_id=1, source_target_pairs={{0,8},{16,24},{32,40},{48,56},{64,72},{80,88},{96,104},{112,120},{... | collective-permute-start | bytes 393224 | tf_op jit(solution)/shard_map/ppermute | solution.py:398

commit v5 on v4

--- a/solution.py
+++ b/solution.py
@@ -44,8 +44,8 @@
         pivot = entry(values, extent, c, c) + RIDGE
         for k in range(c):
             pivot = pivot - low[c][k] * low[c][k]
-        low[c][c] = jnp.sqrt(pivot)
-        inv[c] = 1.0 / low[c][c]
+        inv[c] = lax.rsqrt(pivot)
+        low[c][c] = pivot * inv[c]
         for r in range(c + 1, extent):
             value = entry(values, extent, r, c)
             for k in range(c):

time: 73.5 us -> 73.4 us (level)
  no operation moved by 1% of the time
where the time goes in v5:
time: 73.4 us; the launch traced here: 73.2 us
  blocking collectives  59.1 us (81%)
  Pallas kernels  7.44 us (10%)
  starting transfers between devices  4.86 us (7%)
  waiting for transfers between devices  1.03 us (1%)
    all_to_all x1, blocking collectives, per_device(): lax.all_to_all(z, ('pair', 'grp'), split_axis=0, concat_axis=0, tiled=True)  25 us
    all_to_all x1, blocking collectives, per_device(): lax.all_to_all(copies.reshape(LO, 1, LANES), (*TM, 'grp'), split_axis=0,...  19.8 us
    all_to_all x1, blocking collectives, per_device(): lax.all_to_all(copies, 'grp', split_axis=0, concat_axis=0, tiled=True)  14.3 us
    pallas_call x5, Pallas kernels, call(): pl.pallas_call(kernel, out_shape=out_shape, in_specs=[given] * len(args),...  7.44 us
    ppermute x3, starting transfers between devices, paired(): lax.ppermute(x, TM, [(i, i + 1) for i in low] + [(i + 1, i) for i in low])  4.86 us
  transfers between devices with their start and end apart: 3, of which 1 were waited for; matrix products, arithmetic and copies ran while one was open for 0% of the time, Pallas kernels for 2%

profile of v5, /device:TPU:1, one launch (start us, length us, event | category | flops | bytes accessed | tf_op | source)
XLA Modules:
  0.0 73.2 jit_solution(1679340091346071087)
XLA Ops:
  0.6 2.6 %shard_map.138 = (f32[24,128]{1,0:T(8,128)S(1)}, f32[8,32,128]{2,1,0:T(8,128)S(1)}, f32[24,128]{1,0:T(8,128)S(1)}, f32[3,24,128]{2,1,0:T(8,128)S(1)}, f32[24,128...) custom-call(f32[24,128]{1,0:T(8,128)} %bitcast.28, ...), custom_call_target="tpu_custom_call" | custom-call | flops 16777216 | bytes 1048576 | tf_op jit(solution)/shard_map/pallas_call | solution.py:405
  3.2 14.3 %all_to_all.15 = f32[8,32,128]{2,1,0:T(8,128)S(1)} all-to-all(f32[8,32,128]{2,1,0:T(8,128)S(1)} %get-tuple-element.25), channel_id=1, replica_groups=mesh['pair'=16,'core'=2,'grp'=8] {'grp'}, dimensions={0} | all-to-all | bytes 262144 | tf_op jit(solution)/shard_map/all_to_all | solution.py:441
  17.6 4.2 %collective-permute-start.1 = (f32[32,128]{1,0:T(8,128)S(1)}, f32[32,128]{1,0:T(8,128)S(1)}, u32[]{:S(2)}, u32[]{:S(2)}) collective-permute-start(f32[32,128]{1,0:T(8,128)S(1)} %reduce_sum.9.own), channel_id=1, source_target_pairs={{8,16},{24,32},{40,48},{56,64},{72,80},{88,96},{104,112},{120,128}... | collective-permute-start | bytes 49160 | tf_op jit(solution)/shard_map/ppermute | solution.py:398
  21.8 0.1 collective-permute-start
  21.9 1.3 %shard_map.139 = (f32[256,128]{1,0:T(8,128)S(1)}, f32[256,128]{1,0:T(8,128)S(1)}, bf16[256,3072]{1,0:T(8,128)(2,1)S(1)}) custom-call(f32[24,128]{1,0:T(8,128)S(1)} %get-tuple-element.30.w, f32[6,24,128]{2,1,0:T(8,128)S(1)} %get-tuple-element.31.cp, s32[24,128]{1,0:T(8,128)S(1)} %get-tuple-element.32.ci, f32[4,24,128]{2,1,0:T(8,128)S(1)} %get-tuple-element.33.gp, ...), custom_call_target="tpu_custom_call" | custom-call | flops 134217728 | bytes 1048576 | tf_op jit(solution)/shard_map/pallas_call | solution.py:405
  23.1 0.0 collective-permute-done.1.outside
  23.2 0.0 collective-permute-done.inside
  23.2 1.3 %shard_map.140 = (f32[24,128]{1,0:T(8,128)S(1)}, f32[3,96]{1,0:T(4,128)}, f32[256,128]{1,0:T(8,128)S(1)}, f32[256,128]{1,0:T(8,128)S(1)}) custom-call(f32[32,128]{1,0:T(8,128)S(1)} %reduce_sum.9.own, f32[32,128]{1,0:T(8,128)S(1)} %collective-permute-done.inside, f32[32,128]{1,0:T(8,128)S(1)} %collective-permute-done.1.outside, ...), custom_call_target="tpu_custom_call" | custom-call | flops 16777216 | bytes 1048576 | tf_op jit(solution)/shard_map/pallas_call | solution.py:405
  24.5 0.6 collective-permute-start.2
  25.1 1.0 %collective-permute-done.2 = f32[256,128]{1,0:T(8,128)S(1)} collective-permute-done((f32[256,128]{1,0:T(8,128)S(1)}, f32[256,128]{1,0:T(8,128)S(1)}, u32[]{:S(2)}, u32[]{:S(2)}) %collective-permute-start.2) | collective-permute-done | bytes 131104 | tf_op jit(solution)/shard_map/ppermute | solution.py:398
  26.1 25.0 %all_to_all.16 = f32[128,2,128]{2,1,0:T(2,128)S(1)} all-to-all(f32[128,2,128]{2,1,0:T(2,128)S(1)} %bitcast.22), channel_id=1, replica_groups=mesh['pair'=16,'core'=2,'grp'=8] {'pair','grp'}, dimensions={0} | all-to-all | bytes 262144 | tf_op jit(solution)/shard_map/all_to_all | solution.py:458
  51.1 0.7 %shard_map.141 = (f32[256,128]{1,0:T(8,128)S(1)}, f32[8,128]{1,0:T(8,128)S(1)}, f32[1,4]{1,0:T(1,128)}) custom-call(f32[256,128]{1,0:T(8,128)S(1)} %bitcast.20), custom_call_target="tpu_custom_call" | custom-call | bytes 1048576 | tf_op jit(solution)/shard_map/pallas_call | solution.py:405
  51.8 19.8 %all_to_all.17 = f32[256,1,128]{2,1,0:T(1,128)S(1)} all-to-all(f32[256,1,128]{2,1,0:T(1,128)S(1)} %bitcast.21), channel_id=1, replica_groups=mesh['pair'=16,'core'=2,'grp'=8] {'pair','core','grp'}, dimensions={0} | all-to-all | bytes 262144 | tf_op jit(solution)/shard_map/all_to_all | solution.py:465
  71.6 1.5 %shard_map.142 = (f32[24,128]{1,0:T(8,128)}, f32[6,2048]{1,0:T(8,128)}) custom-call(f32[256,128]{1,0:T(8,128)S(1)} %bitcast.19, f32[24,128]{1,0:T(8,128)S(1)} %get-tuple-element.40.second, f32[6,24,128]{2,1,0:T(8,128)S(1)} %get-tuple-element.31.cp, s32[24,128]{1,0:T(8,128)S(1)} %get-tuple-element.32.ci, f32[4,24,128]{2,1,0:T(8,128)S(1)} %get-tuple-element.33.gp, ...), custom_call_target="tpu_custom_call" | custom-call | bytes 1048576 | tf_op jit(solution)/shard_map/pallas_call | solution.py:405
  (2 shorter events, 0.0 us)
Async XLA Ops:
  17.6 5.6 %collective-permute-start.1 = (f32[32,128]{1,0:T(8,128)S(1)}, f32[32,128]{1,0:T(8,128)S(1)}, u32[]{:S(2)}, u32[]{:S(2)}) collective-permute-start(f32[32,128]{1,0:T(8,128)S(1)} %reduce_sum.9.own), channel_id=1, source_target_pairs={{8,16},{24,32},{40,48},{56,64},{72,80},{88,96},{104,112},{120,128}... | collective-permute-start | bytes 49160 | tf_op jit(solution)/shard_map/ppermute | solution.py:398
  21.8 1.4 %collective-permute-start = (f32[32,128]{1,0:T(8,128)S(1)}, f32[32,128]{1,0:T(8,128)S(1)}, u32[]{:S(2)}, u32[]{:S(2)}) collective-permute-start(f32[32,128]{1,0:T(8,128)S(1)} %reduce_sum.9.own), channel_id=1, source_target_pairs={{0,8},{16,24},{32,40},{48,56},{64,72},{80,88},{96,104},{112,120},{... | collective-permute-start | bytes 49160 | tf_op jit(solution)/shard_map/ppermute | solution.py:398
  24.5 1.5 %collective-permute-start.2 = (f32[256,128]{1,0:T(8,128)S(1)}, f32[256,128]{1,0:T(8,128)S(1)}, u32[]{:S(2)}, u32[]{:S(2)}) collective-permute-start(f32[256,128]{1,0:T(8,128)S(1)} %get-tuple-element.38), channel_id=1, source_target_pairs={{0,8},{16,24},{32,40},{48,56},{64,72},{80,88},{96,104},{112,120},{... | collective-permute-start | bytes 393224 | tf_op jit(solution)/shard_map/ppermute | solution.py:398
